TPU v7x, 32 devices: a whole 2x2x4 slice. The times are simulated.
32 devices in a mesh: expert: 8 (over z, x), dp: 4 (over y, core).
Axes of the slice: x: 2, y: 2, z: 4, core: 2. Of those that a mesh axis runs over, the one named last changes fastest.
Arguments:
- tokens: bfloat16 [8192, 5120], P(('dp', 'expert')), parts along dimension 0, may hold values from -6 to 6
- router_logit: float32 [8192], P(('dp', 'expert')), parts along dimension 0, may hold values from 0 to 3
- expert_id: int32 [8192], P(('dp', 'expert')), parts along dimension 0, may hold values from 0 to 7, as said below
- token_slot: int32 [8192], P(('dp', 'expert')), parts along dimension 0, may hold values from 0 to 63, as said below
- keep: int32 [8192], P(('dp', 'expert')), parts along dimension 0, may hold values 0 or 1
- overflow_host: int32 [8, 32], replicated, may hold values from 0 to 7, as said below
- expert_gate: bfloat16 [8, 5120, 256], P('expert'), may hold values from -0.125 to 0.125
- expert_up: bfloat16 [8, 5120, 256], P('expert'), may hold values from -0.125 to 0.125
- expert_down: bfloat16 [8, 256, 5120], P('expert'), may hold values from -0.375 to 0.375
- shared_gate: bfloat16 [5120, 64], replicated, may hold values from -0.078125 to 0.078125
- shared_up: bfloat16 [5120, 64], replicated, may hold values from -0.078125 to 0.078125
- shared_down: bfloat16 [64, 5120], replicated, may hold values from -0.1875 to 0.1875
Outputs:
- moe_out: bfloat16 [8192, 5120], P(('dp', 'expert')), parts along dimension 0
There are 4 independent parts, one for each index of `dp`. A program takes and returns all parts, laid end to end along the dimension named above; an argument that names none is the same for every part. Nothing has to cross between parts.
Inputs may be any that keep to these rules, and one draw needn't show every extreme that they name: `expert_id`: among the 256 tokens of one device at most 64 name the same expert; some experts are named by exactly 64 tokens of every device. `token_slot`: if c tokens of one device name the same expert, their slots are 0 to c - 1, each once. overflow_host[e, j] is e + 1 or e - 1, taken modulo 8.
All inputs are finite; a program needn't handle non-finite values. No bound on the sum of `keep` on one device may be relied on, other than what follows from the above.
Results may differ from a plain program's by a relative error of at most 0.007.
Values may be sent and summed in bfloat16 or wider, within the bound.
A program may use at most 128 MiB of HBM per device.

v0:
```python
import functools

import jax
import jax.numpy as jnp
from jax import lax
from jax.experimental import pallas as pl
from jax.experimental.pallas import tpu as pltpu
from jax.sharding import PartitionSpec as P

MESH = pl.DeviceIdType.MESH


def expert_ffn(inputs, w_gate, w_up, w_down):
    flat_rows = inputs.reshape(-1, inputs.shape[-1])
    gate_out = jnp.dot(flat_rows, w_gate, preferred_element_type=jnp.float32)
    up_out = jnp.dot(flat_rows, w_up, preferred_element_type=jnp.float32)
    hidden = (jax.nn.silu(gate_out) * up_out).astype(jnp.bfloat16)
    result = jnp.dot(hidden, w_down, preferred_element_type=jnp.float32).astype(jnp.bfloat16)
    return result.reshape(inputs.shape)


def flip(index, step, count):
    out, bit = 0, 1
    while bit < count:
        out = out + bit * lax.rem(index // bit + step // bit, 2)
        bit *= 2
    return out


def moe_kernel(
    dps,
    experts,
    groups,
    home_pick,
    pool_pick,
    side_out,
    need_ref,
    scale_ref,
    tok_ref,
    wg_hbm,
    wu_hbm,
    wd_hbm,
    sg_ref,
    su_ref,
    home_ret,
    pool_ret,
    shared_ref,
    need_max,
    need_all,
    routed_in,
    home_out,
    pool_out,
    home_in,
    home_res,
    pool_in,
    pool_res,
    pool_part,
    pool_comb,
    side_in,
    wg,
    wu,
    wd,
    w_sem,
    own_sem,
    ns_sem,
    nr_sem,
    hs_sem,
    hr_sem,
    rs_sem,
    rr_sem,
    zs_sem,
    zr_sem,
    ms_sem,
    mr_sem,
    xs_sem,
    xr_sem,
    ps_sem,
    pr_sem,
    cs_sem,
    cr_sem,
):
    my_dp = lax.axis_index("dp")
    e = lax.axis_index("expert")
    g = e // 2
    p = e - 2 * g
    partner = e + 1 - 2 * p
    total = dps * experts
    me = my_dp * experts + e

    barrier = pltpu.get_barrier_semaphore()

    @pl.loop(1, total)
    def _(k):
        there = lax.rem(me + k, total)
        pl.semaphore_signal(
            barrier,
            inc=1,
            device_id={"dp": there // experts, "expert": lax.rem(there, experts)},
            device_id_type=MESH,
        )

    weights = [
        pltpu.make_async_copy(a, b, w_sem.at[i])
        for i, (a, b) in enumerate(((wg_hbm, wg), (wu_hbm, wu), (wd_hbm, wd)))
    ]
    own = [
        pltpu.make_async_copy(home_out.at[e], home_in.at[e], own_sem.at[0]),
        pltpu.make_async_copy(pool_out.at[g], pool_in.at[0, g], own_sem.at[1]),
        pltpu.make_async_copy(side_out.at[g], side_in.at[g], own_sem.at[2]),
        pltpu.make_async_copy(need_ref, need_all.at[me], own_sem.at[3]),
    ]

    def remote(src, dst, send, recv, to):
        return pltpu.make_async_remote_copy(
            src_ref=src,
            dst_ref=dst,
            send_sem=send,
            recv_sem=recv,
            device_id={"expert": to},
            device_id_type=MESH,
        )

    def n_copy(k):
        there = lax.rem(me + k, total)
        return pltpu.make_async_remote_copy(
            src_ref=need_ref,
            dst_ref=need_all.at[me],
            send_sem=ns_sem.at[k],
            recv_sem=nr_sem.at[k],
            device_id={"dp": there // experts, "expert": lax.rem(there, experts)},
            device_id_type=MESH,
        )

    def z_copy(k):
        to = flip(g, k, groups)
        return remote(pool_out.at[to], pool_in.at[0, g], zs_sem.at[k], zr_sem.at[k], 2 * to + p)

    def m_copy(k):
        to = flip(g, k, groups)
        return remote(side_out.at[to], side_in.at[g], ms_sem.at[k], mr_sem.at[k], 2 * to + p)

    def h_copy(k):
        to = flip(e, k, experts)
        return remote(home_out.at[to], home_in.at[e], hs_sem.at[k], hr_sem.at[k], to)

    def x_copy(k):
        origin = flip(g, k, groups)
        return remote(
            pool_in.at[0, origin],
            pool_in.at[1, flip(g, k, groups)],
            xs_sem.at[k],
            xr_sem.at[k],
            partner,
        )

    def p_copy(k):
        origin = flip(g, k, groups)
        return remote(
            pool_res.at[origin], pool_part.at[origin], ps_sem.at[k], pr_sem.at[k], partner
        )

    def c_copy(k):
        origin = flip(g, k, groups)
        return remote(
            pool_comb.at[origin], pool_ret.at[g], cs_sem.at[k], cr_sem.at[k], 2 * origin + p
        )

    def r_copy(k):
        origin = flip(e, k, experts)
        return remote(home_res.at[origin], home_ret.at[e], rs_sem.at[k], rr_sem.at[k], origin)

    def rows_of(pick):
        return jnp.dot(pick, routed_in[...], preferred_element_type=jnp.float32).astype(jnp.bfloat16)

    routed_in[...] = (tok_ref[...].astype(jnp.float32) * scale_ref[...]).astype(jnp.bfloat16)

    pl.semaphore_wait(barrier, total - 1)

    @pl.loop(1, groups + 1)
    def _(i):
        k = groups - i
        to = flip(g, k, groups)
        pool_out[to] = rows_of(pool_pick[to])

        @pl.when(i > 1)
        def _():
            z_copy(k + 1).start()
            m_copy(k + 1).start()

    @pl.loop(1, experts + 1)
    def _(i):
        k = experts - i
        to = flip(e, k, experts)
        home_out[to] = rows_of(home_pick[to])

        @pl.when(i > 1)
        def _():
            h_copy(k + 1).start()

    for copy in own:
        copy.start()
    for copy in weights:
        copy.start()

    @pl.loop(1, total)
    def _(k):
        n_copy(k).start()

    for copy in own:
        copy.wait()
    x_copy(0).start()

    tok = tok_ref[...]
    last = (((1,), (1,)), ((), ()))
    shared_gate = lax.dot_general(tok, sg_ref[...], last, preferred_element_type=jnp.float32)
    shared_up = lax.dot_general(tok, su_ref[...], last, preferred_element_type=jnp.float32)
    shared_ref[...] = (jax.nn.silu(shared_gate) * shared_up).astype(jnp.bfloat16)

    for copy in weights:
        copy.wait()

    def ffn(x):
        gate_out = jnp.dot(x, wg[...], preferred_element_type=jnp.float32)
        up_out = jnp.dot(x, wu[...], preferred_element_type=jnp.float32)
        hidden = (jax.nn.silu(gate_out) * up_out).astype(jnp.bfloat16)
        return jnp.dot(hidden, wd[...], preferred_element_type=jnp.float32).astype(jnp.bfloat16)

    home_res[e] = ffn(home_in[e])
    own_ret = pltpu.make_async_copy(home_res.at[e], home_ret.at[e], own_sem.at[0])
    own_ret.start()

    @pl.loop(1, groups)
    def _(i):
        k = groups - i
        z_copy(k).wait_recv()
        x_copy(k).start()

    def home_block(i):
        k = experts - i
        origin = flip(e, k, experts)
        h_copy(k).wait_recv()
        home_res[origin] = ffn(home_in[origin])
        r_copy(k).start()

    @pl.loop(1, groups + 1)
    def _(i):
        k = groups - i
        origin = flip(g, k, groups)
        x_copy(k).wait_recv()
        pool_res[origin] = ffn(pool_in[1, origin])
        p_copy(k).start()

    @pl.loop(1, groups + 1)
    def _(i):
        k = groups - i
        origin = flip(g, k, groups)
        mine = ffn(pool_in[0, origin])
        p_copy(k).wait_recv()

        @pl.when(k > 0)
        def _():
            m_copy(k).wait_recv()

        here = jnp.abs(side_in[origin][:, :1] - p.astype(jnp.float32)) < 0.5
        pool_comb[origin] = jnp.where(here, mine, pool_part[origin])

        @pl.when(k > 0)
        def _():
            c_copy(k).start()

    own_back = pltpu.make_async_copy(pool_comb.at[g], pool_ret.at[g], own_sem.at[1])
    own_back.start()

    pl.loop(1, experts)(home_block)

    @pl.loop(0, groups)
    def _(k):
        x_copy(k).wait_send()
        p_copy(k).wait_send()

    @pl.loop(1, groups)
    def _(k):
        z_copy(k).wait_send()
        m_copy(k).wait_send()
        c_copy(k).wait()

    @pl.loop(1, total)
    def _(k):
        n_copy(k).wait()

    @pl.loop(1, experts)
    def _(k):
        h_copy(k).wait_send()
        r_copy(k).wait()

    own_ret.wait()
    own_back.wait()
    need_max[...] = jnp.max(need_all[...], axis=0)


def routed_exchange(
    home_pick, pool_pick, side_out, need, scale, tokens, w_gate, w_up, w_down, shared_gate, shared_up
):
    dps, experts = lax.axis_size("dp"), lax.axis_size("expert")
    groups = pool_pick.shape[0]
    width = tokens.shape[1]
    home_shape, pool_shape = home_pick.shape[:2] + (width,), pool_pick.shape[:2] + (width,)
    bf16 = jnp.bfloat16
    vmem = pl.BlockSpec(memory_space=pltpu.VMEM)
    anywhere = pl.BlockSpec(memory_space=pl.ANY)
    dma = pltpu.SemaphoreType.DMA
    return pl.pallas_call(
        functools.partial(moe_kernel, dps, experts, groups),
        out_shape=(
            jax.ShapeDtypeStruct(home_shape, bf16),
            jax.ShapeDtypeStruct(pool_shape, bf16),
            jax.ShapeDtypeStruct((tokens.shape[0], shared_gate.shape[0]), bf16),
            jax.ShapeDtypeStruct(need.shape, need.dtype),
        ),
        in_specs=[vmem] * 6 + [anywhere] * 3 + [vmem] * 2,
        out_specs=(vmem,) * 4,
        scratch_shapes=[
            pltpu.VMEM((dps * experts,) + need.shape, need.dtype),
            pltpu.VMEM(tokens.shape, bf16),
            pltpu.VMEM(home_shape, bf16),
            pltpu.VMEM(pool_shape, bf16),
            pltpu.VMEM(home_shape, bf16),
            pltpu.VMEM(home_shape, bf16),
            pltpu.VMEM((2,) + pool_shape, bf16),
            pltpu.VMEM(pool_shape, bf16),
            pltpu.VMEM(pool_shape, bf16),
            pltpu.VMEM(pool_shape, bf16),
            pltpu.VMEM(side_out.shape, jnp.float32),
            pltpu.VMEM(w_gate.shape, bf16),
            pltpu.VMEM(w_up.shape, bf16),
            pltpu.VMEM(w_down.shape, bf16),
            dma((3,)),
            dma((4,)),
        ]
        + [dma((dps * experts,))] * 2
        + [dma((experts,))] * 4
        + [dma((groups,))] * 10,
        compiler_params=pltpu.CompilerParams(
            collective_id=0, has_side_effects=True, vmem_limit_bytes=60 * 1024 * 1024
        ),
        name="moe",
    )(home_pick, pool_pick, side_out, need, scale, tokens, w_gate, w_up, w_down, shared_gate, shared_up)


def split_columns(total, step=256):
    out, at = [], 0
    while at < total:
        out.append((at, min(step, total - at)))
        at += step
    return out


def slab_kernel(
    dps,
    experts,
    groups,
    need_ref,
    home_pick,
    pool_pick,
    back_ref,
    sel_ref,
    scale_ref,
    tok_ref,
    wg_hbm,
    wu_hbm,
    wd_hbm,
    sg_ref,
    su_ref,
    out_ref,
    shared_ref,
    need_max,
    need_all,
    routed_in,
    home_out,
    pool_out,
    home_in,
    pool_in,
    res,
    ret,
    wg,
    wu,
    slab,
    sel_all,
    h_all,
    spread,
    stage,
    w_sem,
    own_sem,
    ns_sem,
    nr_sem,
    hs_sem,
    hr_sem,
    rs_sem,
    rr_sem,
    zs_sem,
    zr_sem,
    xs_sem,
    xr_sem,
    ls_sem,
    lr_sem,
    gs_sem,
    gr_sem,
    os_sem,
    or_sem,
    vs_sem,
    vr_sem,
    ss_sem,
    sr_sem,
):
    my_dp = lax.axis_index("dp")
    e = lax.axis_index("expert")
    g = e // 2
    p = e - 2 * g
    partner = e + 1 - 2 * p
    total = dps * experts
    me = my_dp * experts + e
    members = 2 * dps
    j = p * dps + my_dp
    half = groups // 2
    mate = flip(g, 1, groups)
    far_mid = jnp.where(g < half, half, half - 1)
    far_end = flip(far_mid, 1, groups)
    is_mid = (g == half) | (g == half - 1)
    direct = home_pick.shape[1]
    pooled = pool_pick.shape[1]
    rows, width = tok_ref.shape
    hid = wg.shape[1]
    ncols = slab.shape[3]
    chunks = split_columns(ncols)

    barrier = pltpu.get_barrier_semaphore()

    @pl.loop(1, total)
    def _(k):
        there = lax.rem(me + k, total)
        pl.semaphore_signal(
            barrier,
            inc=1,
            device_id={"dp": there // experts, "expert": lax.rem(there, experts)},
            device_id_type=MESH,
        )

    def columns(member, at=0, count=ncols):
        return pl.ds(pl.multiple_of(member * ncols + at, 128), count)

    weights = [
        pltpu.make_async_copy(a, b, w_sem.at[i])
        for i, (a, b) in enumerate(((wg_hbm, wg), (wu_hbm, wu)))
    ]
    own_slab = pltpu.make_async_copy(wd_hbm.at[:, columns(j)], slab.at[g, p], w_sem.at[2])
    own = [
        pltpu.make_async_copy(home_out.at[e], home_in.at[e], own_sem.at[0]),
        pltpu.make_async_copy(pool_out.at[g], pool_in.at[g, 0], own_sem.at[1]),
        pltpu.make_async_copy(need_ref, need_all.at[me], own_sem.at[2]),
        pltpu.make_async_copy(sel_ref, sel_all.at[j], own_sem.at[3]),
    ]

    def remote(src, dst, send, recv, to):
        return pltpu.make_async_remote_copy(
            src_ref=src,
            dst_ref=dst,
            send_sem=send,
            recv_sem=recv,
            device_id=to,
            device_id_type=MESH,
        )

    def n_copy(k):
        there = lax.rem(me + k, total)
        to = {"dp": there // experts, "expert": lax.rem(there, experts)}
        return remote(need_ref, need_all.at[me], ns_sem.at[k], nr_sem.at[k], to)

    def z_copy(k):
        to = flip(g, k, groups)
        there = {"expert": 2 * to + p}
        return remote(pool_out.at[to], pool_in.at[g, 0], zs_sem.at[k], zr_sem.at[k], there)

    def h_copy(k):
        to = flip(e, k, experts)
        return remote(home_out.at[to], home_in.at[e], hs_sem.at[k], hr_sem.at[k], {"expert": to})

    def x_copy(k):
        origin = flip(g, k, groups)
        return remote(
            pool_in.at[origin, 0],
            pool_in.at[flip(g, k, groups), 1],
            xs_sem.at[k],
            xr_sem.at[k],
            {"expert": partner},
        )

    def r_copy(k):
        origin = flip(e, k, experts)
        return remote(res.at[origin], ret.at[e], rs_sem.at[k], rr_sem.at[k], {"expert": origin})

    def peer(k):
        m = flip(j, k, members)
        return m, {"dp": lax.rem(m, dps), "expert": 2 * g + m // dps}

    def l_copy(k):
        return remote(sel_ref, sel_all.at[j], ls_sem.at[k], lr_sem.at[k], peer(k)[1])

    def g_copy(k):
        return remote(h_all.at[j], h_all.at[j], gs_sem.at[k], gr_sem.at[k], peer(k)[1])

    def o_copy(k, c):
        at, count = chunks[c]
        m, there = peer(k)
        return remote(
            stage.at[m, :, pl.ds(at, count)],
            out_ref.at[:, columns(j, at, count)],
            os_sem.at[k, c],
            or_sem.at[k, c],
            there,
        )

    def v_copy():
        j_there = (1 - p) * dps + my_dp
        return remote(
            wd_hbm.at[:, columns(j_there)],
            slab.at[g, p],
            vs_sem.at[0],
            vr_sem.at[0],
            {"expert": partner},
        )

    def s_copy(block, c, slot, to):
        at, count = chunks[c]
        part = slab.at[block, :, :, pl.ds(at, count)]
        return remote(part, part, ss_sem.at[slot, c], sr_sem.at[block, c], {"expert": 2 * to + p})

    def rows_of(pick):
        return jnp.dot(pick, routed_in[...], preferred_element_type=jnp.float32).astype(jnp.bfloat16)

    for copy in weights:
        copy.start()
    own_slab.start()
    routed_in[...] = (tok_ref[...].astype(jnp.float32) * scale_ref[...]).astype(jnp.bfloat16)
    res[...] = jnp.zeros_like(res)

    pl.semaphore_wait(barrier, total - 1)

    @pl.loop(1, groups + 1)
    def _(i):
        k = groups - i
        to = flip(g, k, groups)
        pool_out[to] = rows_of(pool_pick[to])

        @pl.when(i > 1)
        def _():
            z_copy(k + 1).start()

    @pl.loop(1, experts + 1)
    def _(i):
        k = experts - i
        to = flip(e, k, experts)
        home_out[to] = rows_of(home_pick[to])

        @pl.when(i > 1)
        def _():
            h_copy(k + 1).start()

    for copy in own:
        copy.start()
    v_copy().start()

    @pl.loop(1, total)
    def _(k):
        n_copy(k).start()

    @pl.loop(1, members)
    def _(k):
        l_copy(k).start()

    for copy in own:
        copy.wait()
    x_copy(0).start()

    tok = tok_ref[...]
    last = (((1,), (1,)), ((), ()))
    shared_gate = lax.dot_general(tok, sg_ref[...], last, preferred_element_type=jnp.float32)
    shared_up = lax.dot_general(tok, su_ref[...], last, preferred_element_type=jnp.float32)
    shared_ref[...] = (jax.nn.silu(shared_gate) * shared_up).astype(jnp.bfloat16)

    own_slab.wait()
    v_copy().wait_recv()
    for c in range(len(chunks)):
        s_copy(g, c, 1, far_mid).start()
        s_copy(g, c, 0, mate).start()

    for copy in weights:
        copy.wait()

    def hidden_of(x):
        gate_out = jnp.dot(x, wg[...], preferred_element_type=jnp.float32)
        up_out = jnp.dot(x, wu[...], preferred_element_type=jnp.float32)
        return (jax.nn.silu(gate_out) * up_out).astype(jnp.bfloat16)

    res[e, :direct, :] = hidden_of(home_in[e])

    @pl.loop(1, groups)
    def _(i):
        k = groups - i
        z_copy(k).wait_recv()
        x_copy(k).start()

    base = (direct + 15) // 16 * 16

    @pl.loop(1, groups + 1)
    def _(i):
        k = groups - i
        origin = flip(g, k, groups)
        x_copy(k).wait_recv()
        both = hidden_of(pool_in[origin].reshape(2 * pooled, width))
        res[2 * origin + p, base : base + pooled, :] = both[:pooled]
        res[2 * origin + 1 - p, base : base + pooled, :] = both[pooled:]

    own_ret = pltpu.make_async_copy(res.at[e], ret.at[e], own_sem.at[0])
    own_ret.start()

    @pl.loop(1, experts)
    def _(i):
        k = experts - i
        origin = flip(e, k, experts)
        h_copy(k).wait_recv()
        res[origin, :direct, :] = hidden_of(home_in[origin])
        r_copy(k).start()

    own_ret.wait()

    @pl.loop(1, experts)
    def _(i):
        r_copy(experts - i).wait_recv()

    found = jnp.dot(
        back_ref[...], ret[...].reshape(-1, hid), preferred_element_type=jnp.float32
    )
    h_all[j] = found.astype(jnp.bfloat16)

    @pl.loop(1, members)
    def _(i):
        g_copy(members - i).start()

    def expand(m):
        values = h_all[m]
        marks = sel_all[m].astype(jnp.float32)
        for x in range(experts):
            mark = marks[:, x : x + 1] > 0.5
            spread[m, :, x * hid : (x + 1) * hid] = jnp.where(mark, values, jnp.zeros_like(values))

    def slab_arrive(c):
        @pl.when(is_mid)
        def _():
            for slot, block in ((2, far_mid), (3, far_end)):
                s_copy(block, c, slot, mate).wait_recv()
                s_copy(block, c, slot, mate).start()

        s_copy(mate, c, 0, mate).wait_recv()

        @pl.when(jnp.logical_not(is_mid))
        def _():
            for block in (far_mid, far_end):
                s_copy(block, c, 2, mate).wait_recv()

    def project(m, c):
        at, count = chunks[c]
        w = slab[:, :, :, at : at + count].reshape(experts * hid, count)
        y = jnp.dot(spread[m], w, preferred_element_type=jnp.float32)
        stage[m, :, at : at + count] = y.astype(jnp.bfloat16)

    expand(j)
    slab_arrive(0)

    @pl.loop(1, members)
    def _(i):
        k = members - i
        l_copy(k).wait_recv()
        g_copy(k).wait_recv()
        expand(peer(k)[0])

    def own_out(c):
        at, count = chunks[c]
        return pltpu.make_async_copy(
            stage.at[j, :, pl.ds(at, count)],
            out_ref.at[:, columns(j, at, count)],
            os_sem.at[0, c],
        )

    for c in range(len(chunks)):
        if c + 1 < len(chunks):
            slab_arrive(c + 1)

        @pl.loop(1, members)
        def _(i):
            k = members - i
            project(peer(k)[0], c)
            o_copy(k, c).start()

        project(j, c)
        own_out(c).start()

    for c in range(len(chunks)):

        @pl.loop(1, members)
        def _(k):
            o_copy(k, c).wait()

        own_out(c).wait()
        s_copy(g, c, 1, far_mid).wait_send()
        s_copy(g, c, 0, mate).wait_send()

        @pl.when(is_mid)
        def _():
            for slot, block in ((2, far_mid), (3, far_end)):
                s_copy(block, c, slot, mate).wait_send()

    v_copy().wait_send()

    @pl.loop(0, groups)
    def _(k):
        x_copy(k).wait_send()

    @pl.loop(1, groups)
    def _(k):
        z_copy(k).wait_send()

    @pl.loop(1, total)
    def _(k):
        n_copy(k).wait()

    @pl.loop(1, members)
    def _(k):
        l_copy(k).wait_send()
        g_copy(k).wait_send()

    @pl.loop(1, experts)
    def _(k):
        h_copy(k).wait_send()
        r_copy(k).wait_send()

    need_max[...] = jnp.max(need_all[...], axis=0)


def slab_exchange(
    need, home_pick, pool_pick, back, sel, scale, tokens, w_gate, w_up, w_down, shared_gate, shared_up
):
    dps, experts = lax.axis_size("dp"), lax.axis_size("expert")
    groups = pool_pick.shape[0]
    rows, width = tokens.shape
    hid = w_gate.shape[1]
    members = 2 * dps
    ncols = width // members
    parts = len(split_columns(ncols))
    direct, pooled = home_pick.shape[1], pool_pick.shape[1]
    cell = (direct + 15) // 16 * 16 + pooled
    bf16 = jnp.bfloat16
    vmem = pl.BlockSpec(memory_space=pltpu.VMEM)
    anywhere = pl.BlockSpec(memory_space=pl.ANY)
    dma = pltpu.SemaphoreType.DMA
    return pl.pallas_call(
        functools.partial(slab_kernel, dps, experts, groups),
        out_shape=(
            jax.ShapeDtypeStruct((rows, width), bf16),
            jax.ShapeDtypeStruct((rows, shared_gate.shape[0]), bf16),
            jax.ShapeDtypeStruct(need.shape, need.dtype),
        ),
        in_specs=[vmem] * 7 + [anywhere] * 3 + [vmem] * 2,
        out_specs=(vmem,) * 3,
        scratch_shapes=[
            pltpu.VMEM((dps * experts,) + need.shape, need.dtype),
            pltpu.VMEM((rows, width), bf16),
            pltpu.VMEM((experts, direct, width), bf16),
            pltpu.VMEM((groups, pooled, width), bf16),
            pltpu.VMEM((experts, direct, width), bf16),
            pltpu.VMEM((groups, 2, pooled, width), bf16),
            pltpu.VMEM((experts, cell, hid), bf16),
            pltpu.VMEM((experts, cell, hid), bf16),
            pltpu.VMEM(w_gate.shape, bf16),
            pltpu.VMEM(w_up.shape, bf16),
            pltpu.VMEM((groups, 2, hid, ncols), bf16),
            pltpu.VMEM((members,) + sel.shape, bf16),
            pltpu.VMEM((members, rows, hid), bf16),
            pltpu.VMEM((members, rows, experts * hid), bf16),
            pltpu.VMEM((members, rows, ncols), bf16),
            dma((3,)),
            dma((4,)),
        ]
        + [dma((dps * experts,))] * 2
        + [dma((experts,))] * 4
        + [dma((groups,))] * 4
        + [dma((members,))] * 4
        + [dma((members, parts))] * 2
        + [dma((1,))] * 2
        + [dma((4, parts)), dma((groups, parts))],
        compiler_params=pltpu.CompilerParams(
            collective_id=1, has_side_effects=True, vmem_limit_bytes=60 * 1024 * 1024
        ),
        name="slab_moe",
    )(need, home_pick, pool_pick, back, sel, scale, tokens, w_gate, w_up, w_down, shared_gate, shared_up)


def body(
    tokens,
    router_logit,
    expert_id,
    token_slot,
    keep,
    overflow_host,
    expert_gate,
    expert_up,
    expert_down,
    shared_gate,
    shared_up,
    shared_down,
):
    experts = lax.axis_size("expert")
    dps = lax.axis_size("dp")
    groups = experts // 2
    my_e = lax.axis_index("expert")
    tok_count, model_width = tokens.shape
    slot_count = 2 * tok_count // experts
    home_count = slot_count // 2
    spill_count = slot_count - home_count
    w_gate, w_up, w_down = expert_gate[0], expert_up[0], expert_down[0]
    token_scale = jax.nn.sigmoid(router_logit) * keep.astype(jnp.float32)
    positions = jnp.arange(tok_count, dtype=jnp.int32)
    is_spill = token_slot >= home_count
    spill_level = jnp.maximum(token_slot - home_count, 0)
    table_index = expert_id * spill_count + spill_level
    table_ids = jnp.arange(experts * spill_count, dtype=jnp.int32)
    host_expert = jnp.sum(
        jnp.where(table_index[:, None] == table_ids[None, :], overflow_host.reshape(1, -1), 0),
        axis=1,
    )
    served = jnp.where(is_spill, host_expert, expert_id)
    kept = keep != 0
    before = positions[None, :] < positions[:, None]

    def rank_of(member, label):
        same = (label[:, None] == label[None, :]) & member[None, :] & before
        return jnp.sum(same.astype(jnp.int32), axis=1)

    direct = max(1, 3 * home_count // 4)
    pooled = home_count
    direct_rank = rank_of(kept, served)
    over = kept & (direct_rank >= direct)
    pool_rank = rank_of(over, served // 2)
    left = over & (pool_rank >= pooled)
    home_cell = jnp.where(kept & ~over, served * direct + direct_rank, -1)
    pool_cell = jnp.where(over & ~left, (served // 2) * pooled + pool_rank, -1)
    home_ids = jnp.arange(experts * direct, dtype=jnp.int32)
    pool_ids = jnp.arange(groups * pooled, dtype=jnp.int32)
    home_pick = (home_ids[:, None] == home_cell[None, :]).astype(jnp.bfloat16)
    pool_pick = (pool_ids[:, None] == pool_cell[None, :]).astype(jnp.bfloat16)
    unserved = jnp.broadcast_to(jnp.max(left.astype(jnp.int32)), (8, 128))
    if groups == 4 and model_width % (2 * dps * 128) == 0:
        cell = (direct + 15) // 16 * 16
        spot = jnp.where(over, cell + pool_rank, direct_rank)
        stride = cell + pooled
        back_cell = jnp.where(kept & ~left, served * stride + spot, -1)
        back_ids = jnp.arange(experts * stride, dtype=jnp.int32)
        back = (back_cell[:, None] == back_ids[None, :]).astype(jnp.bfloat16)
        expert_ids = jnp.arange(128, dtype=jnp.int32)
        sel = (jnp.where(kept & ~left, served, -1)[:, None] == expert_ids[None, :]).astype(
            jnp.bfloat16
        )
        routed, shared_hidden, unserved_all = slab_exchange(
            unserved,
            home_pick.reshape(experts, direct, tok_count),
            pool_pick.reshape(groups, pooled, tok_count),
            back,
            sel,
            token_scale[:, None],
            tokens,
            w_gate,
            w_up,
            w_down,
            shared_gate.T,
            shared_up.T,
        )

        def combined():
            shared = jnp.dot(shared_hidden, shared_down, preferred_element_type=jnp.float32)
            return shared + routed.astype(jnp.float32)

    else:
        side = jnp.sum(
            jnp.where(pool_ids[:, None] == pool_cell[None, :], (served % 2)[None, :], 0), axis=1
        )
        side_out = jnp.broadcast_to(side.astype(jnp.float32)[:, None], (groups * pooled, 128))
        home_ret, pool_ret, shared_hidden, unserved_all = routed_exchange(
            home_pick.reshape(experts, direct, tok_count),
            pool_pick.reshape(groups, pooled, tok_count),
            side_out.reshape(groups, pooled, 128),
            unserved,
            token_scale[:, None],
            tokens,
            w_gate,
            w_up,
            w_down,
            shared_gate.T,
            shared_up.T,
        )

        def combined():
            home_back = (home_cell[:, None] == home_ids[None, :]).astype(jnp.bfloat16)
            pool_back = (pool_cell[:, None] == pool_ids[None, :]).astype(jnp.bfloat16)
            pick = jnp.concatenate([home_back, pool_back, shared_hidden], axis=1)
            source = jnp.concatenate(
                [home_ret.reshape(-1, model_width), pool_ret.reshape(-1, model_width), shared_down],
                axis=0,
            )
            return jnp.dot(pick, source, preferred_element_type=jnp.float32)

    def all_served():
        return combined().astype(jnp.bfloat16)

    def some_left():
        rows = (tokens.astype(jnp.float32) * token_scale[:, None]).astype(jnp.bfloat16)
        lanes = home_count + 2 * spill_count
        to_right = host_expert == (expert_id + 1) % experts
        lane_index = jnp.where(
            is_spill,
            home_count + spill_level + jnp.where(to_right, 0, spill_count),
            token_slot,
        )
        cell_index = served * lanes + lane_index
        source_row = jnp.zeros((experts * lanes,), jnp.int32).at[cell_index].set(positions)
        outgoing = rows[source_row].reshape(experts, lanes, model_width)
        incoming = lax.all_to_all(outgoing, "expert", split_axis=0, concat_axis=0, tiled=True)
        answers = lax.all_to_all(
            expert_ffn(incoming, w_gate, w_up, w_down),
            "expert",
            split_axis=0,
            concat_axis=0,
            tiled=True,
        )
        rest = answers.reshape(-1, model_width)[cell_index].astype(jnp.float32)
        return (combined() + jnp.where(left[:, None], rest, 0.0)).astype(jnp.bfloat16)

    return lax.cond(unserved_all[0, 0] > 0, some_left, all_served)


def solution(mesh):
    return jax.shard_map(
        body,
        mesh=mesh,
        in_specs=(
            P(("dp", "expert"), None),
            P(("dp", "expert")),
            P(("dp", "expert")),
            P(("dp", "expert")),
            P(("dp", "expert")),
            P(),
            P("expert", None, None),
            P("expert", None, None),
            P("expert", None, None),
            P(),
            P(),
            P(),
        ),
        out_specs=P(("dp", "expert"), None),
        check_vma=False,
    )
```

profile of v0, /device:TPU:0, one launch (start us, length us, event | category | flops | bytes accessed | tf_op | source)
XLA Modules:
  0.0 195.2 jit_solution(7126340460636638783)
XLA Ops:
  0.0 0.7 add_maximum_fusion
  0.7 0.8 broadcast_in_dim.39
  1.5 0.2 select_reduce_fusion
  1.6 0.7 and_select_fusion.3
  2.4 0.7 broadcast_compare_fusion.1
  3.0 0.2 convert_reduce_fusion.1
  3.2 0.7 and_select_fusion.2
  3.9 0.2 convert_reduce_fusion
  4.1 0.7 broadcast_select_fusion
  4.8 1.3 add_select_fusion
  6.1 0.8 fusion.13.back_ref
  6.9 0.7 compare_convert_fusion.1.pool_pick
  7.7 1.2 broadcast_in_dim.42.need_ref
  8.9 0.7 fusion.16.sel_ref
  9.6 0.7 compare_convert_fusion.home_pick
  10.3 0.7 divide_multiply_fusion
  11.0 0.8 copy.16.scale_ref
  11.8 0.0 copy-start.1
  11.8 0.0 copy-start.4
  11.9 0.0 copy-start.5
  11.9 177.3 %slab_moe.1 = (bf16[256,5120]{1,0:T(8,128)(2,1)}, bf16[256,64]{1,0:T(8,128)(2,1)S(1)}, s32[8,128]{1,0:T(8,128)}) custom-call(s32[8,128]{1,0:T(8,128)} %broadcast_in_dim.42.need_ref, bf16[8,24,256]{2,1,0:T(8,128)(2,1)} %compare_convert_fusion.home_pick, bf16[4,32,256]{2,1,0:T(8,128)(2,1)} %compare_convert_fusion.1.pool_pick, ...), custom_call_target="tpu_custom_call" | custom-call | tf_op jit(solution)/shard_map/slab_moe/pallas_call | solution.py:765
  189.2 1.2 slice.3
  191.1 0.0 copy-done.1
  191.1 0.0 copy-done.4
  191.1 0.0 copy-done.5
  191.1 4.1 %conditional.7 = (bf16[256,5120]{1,0:T(8,128)(2,1)}) conditional(s32[]{:T(128)} %bitcast.10, (bf16[256,64]{1,0:T(8,128)(2,1)S(1)}, bf16[64,5120]{1,0:T(8,128)(2,1)S(1)}, bf16[256,5120]{1,0:T(8,128)(2,1)}) %tuple.37, (bf16[256,64]{1,0:T(8,128)(2,1)S(1)}, bf16[64,5120]{1,0:T(8,128)(2,1)S(1)}, bf16[256,5120]{1,0:T(8,128)(2,1)}, ...), branch_computations={%region_4.5_spmd, %region_5.7_spmd} | conditional | flops 6224488448 | bytes 159580800
  191.1 4.1 %convolution_add_fusion = bf16[256,5120]{1,0:T(8,128)(2,1)} fusion(bf16[256,64]{1,0:T(8,128)(2,1)S(1)} %get-tuple-element.52, bf16[64,5120]{1,0:T(8,128)(2,1)S(1)} %get-tuple-element.53, bf16[256,5120]{1,0:T(8,128)(2,1)} %get-tuple-element.54), kind=kOutput, calls=%fused_computation.3 | convolution fusion | flops 171704320 | bytes 5931008 | tf_op jit(solution)/shard_map/cond/branch_0_fun/dot_general | solution.py:888
  (3 shorter events, 0.0 us)
Async XLA Ops:
  11.8 179.2 %copy-start.1 = (bf16[64,5120]{1,0:T(8,128)(2,1)S(1)}, bf16[64,5120]{1,0:T(8,128)(2,1)}, u32[]{:S(2)}) copy-start(bf16[64,5120]{1,0:T(8,128)(2,1)} %param.25) | copy-start | bytes 1966084
  11.8 179.2 %copy-start.4 = (s32[256]{0:T(256)S(1)}, s32[256]{0:T(256)}, u32[]{:S(2)}) copy-start(s32[256]{0:T(256)} %param.17) | copy-start | bytes 3076
  11.9 179.2 %copy-start.5 = (s32[256]{0:T(256)S(1)}, s32[256]{0:T(256)}, u32[]{:S(2)}) copy-start(s32[256]{0:T(256)} %param.16) | copy-start | bytes 3076
where the time goes:
time: 196 us; the launch traced here: 195 us
  Pallas kernels  177 us (90%)
  other arithmetic  9.05 us (5%)
  matrix products  4.05 us (2%)
  local copies, waits for them, and re-layouts  3.99 us (2%)
    pallas_call x1, Pallas kernels, slab_exchange(): pl.pallas_call(functools.partial(slab_kernel, dps, experts, groups), out_...  177 us
    dot_general x1, matrix products, combined(): jnp.dot(shared_hidden, shared_down, preferred_element_type=jnp.float32)  4.05 us

commit v1 on v0

--- a/solution.py
+++ b/solution.py
@@ -347,7 +347,7 @@
     )(home_pick, pool_pick, side_out, need, scale, tokens, w_gate, w_up, w_down, shared_gate, shared_up)
 
 
-def split_columns(total, step=256):
+def split_columns(total, step=128):
     out, at = [], 0
     while at < total:
         out.append((at, min(step, total - at)))
@@ -359,23 +359,25 @@
     dps,
     experts,
     groups,
-    need_ref,
-    home_pick,
-    pool_pick,
-    back_ref,
-    sel_ref,
-    scale_ref,
+    direct,
+    pooled,
+    id_ref,
+    slot_ref,
+    keep_ref,
+    logit_ref,
+    table_ref,
     tok_ref,
     wg_hbm,
     wu_hbm,
     wd_hbm,
     sg_ref,
     su_ref,
+    sd_hbm,
     out_ref,
-    shared_ref,
     need_max,
     need_all,
-    routed_in,
+    back,
+    shared_slab,
     home_out,
     pool_out,
     home_in,
@@ -426,10 +428,13 @@
     far_mid = jnp.where(g < half, half, half - 1)
     far_end = flip(far_mid, 1, groups)
     is_mid = (g == half) | (g == half - 1)
-    direct = home_pick.shape[1]
-    pooled = pool_pick.shape[1]
+    mid = is_mid.astype(jnp.int32)
     rows, width = tok_ref.shape
     hid = wg.shape[1]
+    mix = sg_ref.shape[0]
+    spill = table_ref.shape[1]
+    base = (direct + 15) // 16 * 16
+    stride = base + pooled
     ncols = slab.shape[3]
     chunks = split_columns(ncols)
 
@@ -453,11 +458,12 @@
         for i, (a, b) in enumerate(((wg_hbm, wg), (wu_hbm, wu)))
     ]
     own_slab = pltpu.make_async_copy(wd_hbm.at[:, columns(j)], slab.at[g, p], w_sem.at[2])
+    own_mix = pltpu.make_async_copy(
+        sd_hbm.at[:, columns(j)], shared_slab.at[pl.ds(0, mix)], own_sem.at[2]
+    )
     own = [
         pltpu.make_async_copy(home_out.at[e], home_in.at[e], own_sem.at[0]),
         pltpu.make_async_copy(pool_out.at[g], pool_in.at[g, 0], own_sem.at[1]),
-        pltpu.make_async_copy(need_ref, need_all.at[me], own_sem.at[2]),
-        pltpu.make_async_copy(sel_ref, sel_all.at[j], own_sem.at[3]),
     ]
 
     def remote(src, dst, send, recv, to):
@@ -473,7 +479,7 @@
     def n_copy(k):
         there = lax.rem(me + k, total)
         to = {"dp": there // experts, "expert": lax.rem(there, experts)}
-        return remote(need_ref, need_all.at[me], ns_sem.at[k], nr_sem.at[k], to)
+        return remote(need_all.at[me], need_all.at[me], ns_sem.at[k], nr_sem.at[k], to)
 
     def z_copy(k):
         to = flip(g, k, groups)
@@ -503,10 +509,11 @@
         return m, {"dp": lax.rem(m, dps), "expert": 2 * g + m // dps}
 
     def l_copy(k):
-        return remote(sel_ref, sel_all.at[j], ls_sem.at[k], lr_sem.at[k], peer(k)[1])
+        return remote(sel_all.at[j], sel_all.at[j], ls_sem.at[k], lr_sem.at[k], peer(k)[1])
 
     def g_copy(k):
-        return remote(h_all.at[j], h_all.at[j], gs_sem.at[k], gr_sem.at[k], peer(k)[1])
+        block, there = (j, peer(k)[1]) if k == 1 or k % 2 == 0 else (peer(k - 1)[0], peer(1)[1])
+        return remote(h_all.at[block], h_all.at[block], gs_sem.at[k], gr_sem.at[k], there)
 
     def o_copy(k, c):
         at, count = chunks[c]
@@ -534,40 +541,108 @@
         part = slab.at[block, :, :, pl.ds(at, count)]
         return remote(part, part, ss_sem.at[slot, c], sr_sem.at[block, c], {"expert": 2 * to + p})
 
-    def rows_of(pick):
-        return jnp.dot(pick, routed_in[...], preferred_element_type=jnp.float32).astype(jnp.bfloat16)
-
     for copy in weights:
         copy.start()
     own_slab.start()
-    routed_in[...] = (tok_ref[...].astype(jnp.float32) * scale_ref[...]).astype(jnp.bfloat16)
-    res[...] = jnp.zeros_like(res)
-
-    pl.semaphore_wait(barrier, total - 1)
-
-    @pl.loop(1, groups + 1)
+    own_mix.start()
+
+    bf16 = jnp.bfloat16
+
+    def steps(count):
+        return lax.broadcasted_iota(jnp.int32, (count, rows), 0)
+
+    def marks_of(count, label):
+        return jnp.where(steps(count) == label, 1.0, 0.0)
+
+    with jax.named_scope("routing"):
+        ident, slot = id_ref[...], slot_ref[...]
+        kept = keep_ref[...] != 0
+        scale = jax.nn.sigmoid(logit_ref[...]) * keep_ref[...].astype(jnp.float32)
+        levels = marks_of(spill, jnp.maximum(slot - spill, 0)).astype(bf16)
+        table = table_ref[...].astype(jnp.float32).astype(bf16)
+        hosts = jnp.dot(table, levels, preferred_element_type=jnp.float32)
+        host = jnp.sum(hosts * marks_of(experts, ident), axis=0, keepdims=True)
+        served = jnp.where(slot >= spill, host.astype(jnp.int32), ident)
+        order = lax.broadcasted_iota(jnp.int32, (rows, rows), 1)
+        earlier = jnp.where(steps(rows) < order, 1.0, 0.0).astype(bf16)
+
+        def rank_of(count, label):
+            marks = marks_of(count, label)
+            counts = jnp.dot(marks.astype(bf16), earlier, preferred_element_type=jnp.float32)
+            return jnp.sum(marks * counts, axis=0, keepdims=True).astype(jnp.int32)
+
+        direct_rank = rank_of(experts, jnp.where(kept, served, -1))
+        over = kept & (direct_rank >= direct)
+        pool_rank = rank_of(groups, jnp.where(over, served // 2, -1))
+        left = over & (pool_rank >= pooled)
+        home_cell = jnp.where(kept & (direct_rank < direct), served * direct + direct_rank, -1)
+        pool_cell = jnp.where(
+            over & (pool_rank < pooled), (served // 2) * pooled + pool_rank, -1
+        )
+        placed = kept & ((direct_rank < direct) | (pool_rank < pooled))
+
+    def rows_of(cell, first, count):
+        pick = marks_of(count, cell - first)
+        factor = jnp.sum(pick * scale, axis=1, keepdims=True)
+        chosen = jnp.dot(pick.astype(bf16), tok_ref[...], preferred_element_type=jnp.float32)
+        return (chosen * factor).astype(bf16)
+
+    @pl.loop(0, groups)
+    def _(to):
+        with jax.named_scope("pack_pool"):
+            pool_out[to] = rows_of(pool_cell, to * pooled, pooled)
+
+    with jax.named_scope("barrier"):
+        pl.semaphore_wait(barrier, total - 1)
+
+    for k in (3 - mid, 2 + mid, 1):
+        z_copy(k).start()
+
+    v_copy().start()
+
+    @pl.loop(0, experts)
     def _(i):
-        k = groups - i
-        to = flip(g, k, groups)
-        pool_out[to] = rows_of(pool_pick[to])
-
-        @pl.when(i > 1)
-        def _():
-            z_copy(k + 1).start()
-
-    @pl.loop(1, experts + 1)
+        to = flip(e, experts - 1 - i, experts)
+        with jax.named_scope("pack_home"):
+            home_out[to] = rows_of(home_cell, to * direct, direct)
+
+    with jax.named_scope("shared"):
+        tok = tok_ref[...]
+        last = (((1,), (1,)), ((), ()))
+        shared_gate = lax.dot_general(tok, sg_ref[...], last, preferred_element_type=jnp.float32)
+        shared_up = lax.dot_general(tok, su_ref[...], last, preferred_element_type=jnp.float32)
+        lanes = sel_all.shape[2]
+        marks = jnp.transpose(marks_of(lanes, jnp.where(placed, served + mix, -1)))
+        sel_all[j] = marks.astype(bf16)
+        sel_all[j, :, :mix] = (jax.nn.silu(shared_gate) * shared_up).astype(bf16)
+
+    with jax.named_scope("tables"):
+        res[...] = jnp.zeros_like(res)
+        shared_slab[mix:, :] = jnp.zeros((lanes - mix, ncols), bf16)
+        spot = jnp.where(direct_rank < direct, direct_rank, base + pool_rank)
+        cell = jnp.where(placed, served * stride + spot, -1)
+        back[...] = jnp.transpose(marks_of(experts * stride, cell)).astype(bf16)
+        missed = jnp.max(jnp.where(left, 1.0, 0.0), axis=1, keepdims=True)
+        need_all[me] = jnp.broadcast_to(missed, need_all.shape[1:])
+
+    for copy in own[1:]:
+        copy.start()
+    own[1].wait()
+    x_copy(0).start()
+
+    def pool_relay(k):
+        with jax.named_scope("z_wait"):
+            z_copy(k).wait_recv()
+        x_copy(k).start()
+
+    pool_relay(3 - mid)
+
+    @pl.loop(1, experts)
     def _(i):
-        k = experts - i
-        to = flip(e, k, experts)
-        home_out[to] = rows_of(home_pick[to])
-
-        @pl.when(i > 1)
-        def _():
-            h_copy(k + 1).start()
-
-    for copy in own:
-        copy.start()
-    v_copy().start()
+        h_copy(experts - i).start()
+
+    own[0].start()
+    pool_relay(1)
 
     @pl.loop(1, total)
     def _(k):
@@ -577,89 +652,97 @@
     def _(k):
         l_copy(k).start()
 
-    for copy in own:
-        copy.wait()
-    x_copy(0).start()
-
-    tok = tok_ref[...]
-    last = (((1,), (1,)), ((), ()))
-    shared_gate = lax.dot_general(tok, sg_ref[...], last, preferred_element_type=jnp.float32)
-    shared_up = lax.dot_general(tok, su_ref[...], last, preferred_element_type=jnp.float32)
-    shared_ref[...] = (jax.nn.silu(shared_gate) * shared_up).astype(jnp.bfloat16)
-
-    own_slab.wait()
-    v_copy().wait_recv()
+    with jax.named_scope("own_wait"):
+        own[0].wait()
+        own_mix.wait()
+
+    with jax.named_scope("slab_wait"):
+        own_slab.wait()
+        v_copy().wait_recv()
     for c in range(len(chunks)):
-        s_copy(g, c, 1, far_mid).start()
         s_copy(g, c, 0, mate).start()
 
-    for copy in weights:
-        copy.wait()
+    with jax.named_scope("w_wait"):
+        for copy in weights:
+            copy.wait()
 
     def hidden_of(x):
         gate_out = jnp.dot(x, wg[...], preferred_element_type=jnp.float32)
         up_out = jnp.dot(x, wu[...], preferred_element_type=jnp.float32)
         return (jax.nn.silu(gate_out) * up_out).astype(jnp.bfloat16)
 
-    res[e, :direct, :] = hidden_of(home_in[e])
-
-    @pl.loop(1, groups)
+    with jax.named_scope("ffn_own"):
+        res[e, :direct, :] = hidden_of(home_in[e])
+
+    pool_relay(2 + mid)
+
+    @pl.loop(0, groups)
     def _(i):
-        k = groups - i
-        z_copy(k).wait_recv()
-        x_copy(k).start()
-
-    base = (direct + 15) // 16 * 16
-
-    @pl.loop(1, groups + 1)
-    def _(i):
-        k = groups - i
+        k = jnp.where(i == 0, 0, jnp.where(i == 1, 3 - mid, jnp.where(i == 2, 1, 2 + mid)))
         origin = flip(g, k, groups)
-        x_copy(k).wait_recv()
-        both = hidden_of(pool_in[origin].reshape(2 * pooled, width))
-        res[2 * origin + p, base : base + pooled, :] = both[:pooled]
-        res[2 * origin + 1 - p, base : base + pooled, :] = both[pooled:]
+        with jax.named_scope("x_wait"):
+            x_copy(k).wait_recv()
+        with jax.named_scope("ffn_pool"):
+            both = hidden_of(pool_in[origin].reshape(2 * pooled, width))
+            res[2 * origin + p, base : base + pooled, :] = both[:pooled]
+            res[2 * origin + 1 - p, base : base + pooled, :] = both[pooled:]
 
     own_ret = pltpu.make_async_copy(res.at[e], ret.at[e], own_sem.at[0])
     own_ret.start()
 
+    def home_block(k):
+        origin = flip(e, k, experts)
+        with jax.named_scope("h_wait"):
+            h_copy(k).wait_recv()
+        with jax.named_scope("ffn_home"):
+            res[origin, :direct, :] = hidden_of(home_in[origin])
+        r_copy(k).start()
+
     @pl.loop(1, experts)
     def _(i):
-        k = experts - i
-        origin = flip(e, k, experts)
-        h_copy(k).wait_recv()
-        res[origin, :direct, :] = hidden_of(home_in[origin])
-        r_copy(k).start()
+        home_block(jnp.where(i < experts // 2, experts // 2 - i, experts + experts // 2 - 1 - i))
+
+    def far_start(*which):
+        for c in which:
+            s_copy(g, c, 1, far_mid).start()
+
+    far_start(*range(min(2, len(chunks))))
+
+    def slab_step(*which):
+        @pl.when(is_mid)
+        def _():
+            for c in which:
+                with jax.named_scope("slab_relay"):
+                    for slot, block in ((2, far_mid), (3, far_end)):
+                        copy = s_copy(block, c, slot, mate)
+                        copy.wait_recv()
+                        copy.start()
 
     own_ret.wait()
 
-    @pl.loop(1, experts)
-    def _(i):
-        r_copy(experts - i).wait_recv()
-
-    found = jnp.dot(
-        back_ref[...], ret[...].reshape(-1, hid), preferred_element_type=jnp.float32
-    )
-    h_all[j] = found.astype(jnp.bfloat16)
-
-    @pl.loop(1, members)
-    def _(i):
-        g_copy(members - i).start()
+    with jax.named_scope("ret_wait"):
+
+        @pl.loop(1, experts)
+        def _(i):
+            r_copy(experts - i).wait_recv()
+
+    with jax.named_scope("find"):
+        found = jnp.dot(
+            back[...], ret[...].reshape(-1, hid), preferred_element_type=jnp.float32
+        )
+        h_all[j] = found.astype(jnp.bfloat16)
+
+    for k in [*range(members - 2, 0, -2), 1]:
+        g_copy(k).start()
 
     def expand(m):
         values = h_all[m]
         marks = sel_all[m].astype(jnp.float32)
         for x in range(experts):
-            mark = marks[:, x : x + 1] > 0.5
+            mark = marks[:, mix + x : mix + x + 1] > 0.5
             spread[m, :, x * hid : (x + 1) * hid] = jnp.where(mark, values, jnp.zeros_like(values))
 
     def slab_arrive(c):
-        @pl.when(is_mid)
-        def _():
-            for slot, block in ((2, far_mid), (3, far_end)):
-                s_copy(block, c, slot, mate).wait_recv()
-                s_copy(block, c, slot, mate).start()
-
         s_copy(mate, c, 0, mate).wait_recv()
 
         @pl.when(jnp.logical_not(is_mid))
@@ -671,17 +754,32 @@
         at, count = chunks[c]
         w = slab[:, :, :, at : at + count].reshape(experts * hid, count)
         y = jnp.dot(spread[m], w, preferred_element_type=jnp.float32)
+        y += jnp.dot(
+            sel_all[m], shared_slab[:, at : at + count], preferred_element_type=jnp.float32
+        )
         stage[m, :, at : at + count] = y.astype(jnp.bfloat16)
 
-    expand(j)
-    slab_arrive(0)
-
-    @pl.loop(1, members)
-    def _(i):
-        k = members - i
-        l_copy(k).wait_recv()
-        g_copy(k).wait_recv()
-        expand(peer(k)[0])
+    with jax.named_scope("expand"):
+        expand(j)
+
+    def hidden_arrive(k):
+        with jax.named_scope("g_wait"):
+            l_copy(k).wait_recv()
+            g_copy(k).wait_recv()
+        if k % 2 == 0:
+            g_copy(k + 1).start()
+        with jax.named_scope("expand"):
+            expand(peer(k)[0])
+
+    far_start(*range(2, min(3, len(chunks))))
+    for k in [1, *range(2, members, 2)]:
+        hidden_arrive(k)
+        if k == 2:
+            far_start(*range(3, min(4, len(chunks))))
+            slab_step(0)
+    far_start(*range(4, len(chunks)))
+    for k in range(3, members, 2):
+        hidden_arrive(k)
 
     def own_out(c):
         at, count = chunks[c]
@@ -692,23 +790,27 @@
         )
 
     for c in range(len(chunks)):
-        if c + 1 < len(chunks):
-            slab_arrive(c + 1)
+        with jax.named_scope("slab_arrive"):
+            slab_arrive(c)
 
         @pl.loop(1, members)
         def _(i):
             k = members - i
-            project(peer(k)[0], c)
+            with jax.named_scope("project"):
+                project(peer(k)[0], c)
             o_copy(k, c).start()
 
         project(j, c)
         own_out(c).start()
+        if c + 1 < len(chunks):
+            slab_step(c + 1)
 
     for c in range(len(chunks)):
 
         @pl.loop(1, members)
         def _(k):
-            o_copy(k, c).wait()
+            with jax.named_scope("out_wait"):
+                o_copy(k, c).wait()
 
         own_out(c).wait()
         s_copy(g, c, 1, far_mid).wait_send()
@@ -719,7 +821,8 @@
             for slot, block in ((2, far_mid), (3, far_end)):
                 s_copy(block, c, slot, mate).wait_send()
 
-    v_copy().wait_send()
+    with jax.named_scope("v_wait"):
+        v_copy().wait_send()
 
     @pl.loop(0, groups)
     def _(k):
@@ -736,6 +839,8 @@
     @pl.loop(1, members)
     def _(k):
         l_copy(k).wait_send()
+
+    for k in range(1, members):
         g_copy(k).wait_send()
 
     @pl.loop(1, experts)
@@ -743,52 +848,51 @@
         h_copy(k).wait_send()
         r_copy(k).wait_send()
 
-    need_max[...] = jnp.max(need_all[...], axis=0)
+    need_max[0, 0] = jnp.max(need_all[...])
 
 
 def slab_exchange(
-    need, home_pick, pool_pick, back, sel, scale, tokens, w_gate, w_up, w_down, shared_gate, shared_up
+    direct, pooled, expert_id, token_slot, keep, router_logit, table, tokens, weights, shared
 ):
     dps, experts = lax.axis_size("dp"), lax.axis_size("expert")
-    groups = pool_pick.shape[0]
+    groups = experts // 2
     rows, width = tokens.shape
-    hid = w_gate.shape[1]
+    hid = weights[0].shape[1]
     members = 2 * dps
     ncols = width // members
     parts = len(split_columns(ncols))
-    direct, pooled = home_pick.shape[1], pool_pick.shape[1]
     cell = (direct + 15) // 16 * 16 + pooled
     bf16 = jnp.bfloat16
     vmem = pl.BlockSpec(memory_space=pltpu.VMEM)
     anywhere = pl.BlockSpec(memory_space=pl.ANY)
     dma = pltpu.SemaphoreType.DMA
     return pl.pallas_call(
-        functools.partial(slab_kernel, dps, experts, groups),
+        functools.partial(slab_kernel, dps, experts, groups, direct, pooled),
         out_shape=(
             jax.ShapeDtypeStruct((rows, width), bf16),
-            jax.ShapeDtypeStruct((rows, shared_gate.shape[0]), bf16),
-            jax.ShapeDtypeStruct(need.shape, need.dtype),
+            jax.ShapeDtypeStruct((1, 1), jnp.float32),
         ),
-        in_specs=[vmem] * 7 + [anywhere] * 3 + [vmem] * 2,
-        out_specs=(vmem,) * 3,
+        in_specs=[vmem] * 6 + [anywhere] * 3 + [vmem] * 2 + [anywhere],
+        out_specs=(vmem, pl.BlockSpec(memory_space=pltpu.SMEM)),
         scratch_shapes=[
-            pltpu.VMEM((dps * experts,) + need.shape, need.dtype),
-            pltpu.VMEM((rows, width), bf16),
+            pltpu.VMEM((dps * experts, 8, 128), jnp.float32),
+            pltpu.VMEM((rows, experts * cell), bf16),
+            pltpu.VMEM((128, ncols), bf16),
             pltpu.VMEM((experts, direct, width), bf16),
             pltpu.VMEM((groups, pooled, width), bf16),
             pltpu.VMEM((experts, direct, width), bf16),
             pltpu.VMEM((groups, 2, pooled, width), bf16),
             pltpu.VMEM((experts, cell, hid), bf16),
             pltpu.VMEM((experts, cell, hid), bf16),
-            pltpu.VMEM(w_gate.shape, bf16),
-            pltpu.VMEM(w_up.shape, bf16),
+            pltpu.VMEM((width, hid), bf16),
+            pltpu.VMEM((width, hid), bf16),
             pltpu.VMEM((groups, 2, hid, ncols), bf16),
-            pltpu.VMEM((members,) + sel.shape, bf16),
+            pltpu.VMEM((members, rows, 128), bf16),
             pltpu.VMEM((members, rows, hid), bf16),
             pltpu.VMEM((members, rows, experts * hid), bf16),
             pltpu.VMEM((members, rows, ncols), bf16),
             dma((3,)),
-            dma((4,)),
+            dma((3,)),
         ]
         + [dma((dps * experts,))] * 2
         + [dma((experts,))] * 4
@@ -801,7 +905,74 @@
             collective_id=1, has_side_effects=True, vmem_limit_bytes=60 * 1024 * 1024
         ),
         name="slab_moe",
-    )(need, home_pick, pool_pick, back, sel, scale, tokens, w_gate, w_up, w_down, shared_gate, shared_up)
+    )(
+        *(v.reshape(1, rows) for v in (expert_id, token_slot, keep, router_logit)),
+        table,
+        tokens,
+        *weights,
+        shared[0].T,
+        shared[1].T,
+        shared[2],
+    )
+
+
+def slab_body(direct, pooled, args):
+    tokens, router_logit, expert_id, token_slot, keep, table = args[:6]
+    weights = tuple(w[0] for w in args[6:9])
+    shared_gate, shared_up, shared_down = args[9:]
+    out, need = slab_exchange(
+        direct,
+        pooled,
+        expert_id,
+        token_slot,
+        keep,
+        router_logit,
+        table,
+        tokens,
+        weights,
+        args[9:],
+    )
+
+    def some_left():
+        experts = lax.axis_size("expert")
+        count, width = tokens.shape
+        spill = table.shape[1]
+        scale = jax.nn.sigmoid(router_logit) * keep.astype(jnp.float32)
+        positions = jnp.arange(count, dtype=jnp.int32)
+        is_spill = token_slot >= spill
+        level = jnp.maximum(token_slot - spill, 0)
+        host = table[expert_id, level]
+        served = jnp.where(is_spill, host, expert_id)
+        kept = keep != 0
+        before = positions[None, :] < positions[:, None]
+
+        def rank_of(member, label):
+            same = (label[:, None] == label[None, :]) & member[None, :] & before
+            return jnp.sum(same.astype(jnp.int32), axis=1)
+
+        over = kept & (rank_of(kept, served) >= direct)
+        left = over & (rank_of(over, served // 2) >= pooled)
+        rows = (tokens.astype(jnp.float32) * scale[:, None]).astype(jnp.bfloat16)
+        lanes = 3 * spill
+        to_right = host == (expert_id + 1) % experts
+        lane_index = jnp.where(
+            is_spill, spill + level + jnp.where(to_right, 0, spill), token_slot
+        )
+        cell_index = served * lanes + lane_index
+        source_row = jnp.zeros((experts * lanes,), jnp.int32).at[cell_index].set(positions)
+        outgoing = rows[source_row].reshape(experts, lanes, width)
+        incoming = lax.all_to_all(outgoing, "expert", split_axis=0, concat_axis=0, tiled=True)
+        answers = lax.all_to_all(
+            expert_ffn(incoming, *weights), "expert", split_axis=0, concat_axis=0, tiled=True
+        )
+        rest = answers.reshape(-1, width)[cell_index].astype(jnp.float32)
+        gate = jnp.dot(tokens, shared_gate, preferred_element_type=jnp.float32)
+        up = jnp.dot(tokens, shared_up, preferred_element_type=jnp.float32)
+        hidden = (jax.nn.silu(gate) * up).astype(jnp.bfloat16)
+        common = jnp.dot(hidden, shared_down, preferred_element_type=jnp.float32)
+        return jnp.where(left[:, None], (common + rest).astype(jnp.bfloat16), out)
+
+    return lax.cond(need[0, 0] > 0, some_left, lambda: out)
 
 
 def body(
@@ -821,11 +992,18 @@
     experts = lax.axis_size("expert")
     dps = lax.axis_size("dp")
     groups = experts // 2
-    my_e = lax.axis_index("expert")
     tok_count, model_width = tokens.shape
     slot_count = 2 * tok_count // experts
     home_count = slot_count // 2
     spill_count = slot_count - home_count
+    direct = max(1, 3 * home_count // 4)
+    pooled = home_count
+    narrow = shared_gate.shape[1] + experts <= 128 and spill_count == home_count
+    even = dps in (2, 4, 8) and model_width % (2 * dps * 128) == 0
+    if groups == 4 and even and narrow:
+        args = (tokens, router_logit, expert_id, token_slot, keep, overflow_host)
+        args += (expert_gate, expert_up, expert_down, shared_gate, shared_up, shared_down)
+        return slab_body(direct, pooled, args)
     w_gate, w_up, w_down = expert_gate[0], expert_up[0], expert_down[0]
     token_scale = jax.nn.sigmoid(router_logit) * keep.astype(jnp.float32)
     positions = jnp.arange(tok_count, dtype=jnp.int32)
@@ -845,8 +1023,6 @@
         same = (label[:, None] == label[None, :]) & member[None, :] & before
         return jnp.sum(same.astype(jnp.int32), axis=1)
 
-    direct = max(1, 3 * home_count // 4)
-    pooled = home_count
     direct_rank = rank_of(kept, served)
     over = kept & (direct_rank >= direct)
     pool_rank = rank_of(over, served // 2)
@@ -858,64 +1034,33 @@
     home_pick = (home_ids[:, None] == home_cell[None, :]).astype(jnp.bfloat16)
     pool_pick = (pool_ids[:, None] == pool_cell[None, :]).astype(jnp.bfloat16)
     unserved = jnp.broadcast_to(jnp.max(left.astype(jnp.int32)), (8, 128))
-    if groups == 4 and model_width % (2 * dps * 128) == 0:
-        cell = (direct + 15) // 16 * 16
-        spot = jnp.where(over, cell + pool_rank, direct_rank)
-        stride = cell + pooled
-        back_cell = jnp.where(kept & ~left, served * stride + spot, -1)
-        back_ids = jnp.arange(experts * stride, dtype=jnp.int32)
-        back = (back_cell[:, None] == back_ids[None, :]).astype(jnp.bfloat16)
-        expert_ids = jnp.arange(128, dtype=jnp.int32)
-        sel = (jnp.where(kept & ~left, served, -1)[:, None] == expert_ids[None, :]).astype(
-            jnp.bfloat16
-        )
-        routed, shared_hidden, unserved_all = slab_exchange(
-            unserved,
-            home_pick.reshape(experts, direct, tok_count),
-            pool_pick.reshape(groups, pooled, tok_count),
-            back,
-            sel,
-            token_scale[:, None],
-            tokens,
-            w_gate,
-            w_up,
-            w_down,
-            shared_gate.T,
-            shared_up.T,
-        )
-
-        def combined():
-            shared = jnp.dot(shared_hidden, shared_down, preferred_element_type=jnp.float32)
-            return shared + routed.astype(jnp.float32)
-
-    else:
-        side = jnp.sum(
-            jnp.where(pool_ids[:, None] == pool_cell[None, :], (served % 2)[None, :], 0), axis=1
-        )
-        side_out = jnp.broadcast_to(side.astype(jnp.float32)[:, None], (groups * pooled, 128))
-        home_ret, pool_ret, shared_hidden, unserved_all = routed_exchange(
-            home_pick.reshape(experts, direct, tok_count),
-            pool_pick.reshape(groups, pooled, tok_count),
-            side_out.reshape(groups, pooled, 128),
-            unserved,
-            token_scale[:, None],
-            tokens,
-            w_gate,
-            w_up,
-            w_down,
-            shared_gate.T,
-            shared_up.T,
-        )
-
-        def combined():
-            home_back = (home_cell[:, None] == home_ids[None, :]).astype(jnp.bfloat16)
-            pool_back = (pool_cell[:, None] == pool_ids[None, :]).astype(jnp.bfloat16)
-            pick = jnp.concatenate([home_back, pool_back, shared_hidden], axis=1)
-            source = jnp.concatenate(
-                [home_ret.reshape(-1, model_width), pool_ret.reshape(-1, model_width), shared_down],
-                axis=0,
-            )
-            return jnp.dot(pick, source, preferred_element_type=jnp.float32)
+    side = jnp.sum(
+        jnp.where(pool_ids[:, None] == pool_cell[None, :], (served % 2)[None, :], 0), axis=1
+    )
+    side_out = jnp.broadcast_to(side.astype(jnp.float32)[:, None], (groups * pooled, 128))
+    home_ret, pool_ret, shared_hidden, unserved_all = routed_exchange(
+        home_pick.reshape(experts, direct, tok_count),
+        pool_pick.reshape(groups, pooled, tok_count),
+        side_out.reshape(groups, pooled, 128),
+        unserved,
+        token_scale[:, None],
+        tokens,
+        w_gate,
+        w_up,
+        w_down,
+        shared_gate.T,
+        shared_up.T,
+    )
+
+    def combined():
+        home_back = (home_cell[:, None] == home_ids[None, :]).astype(jnp.bfloat16)
+        pool_back = (pool_cell[:, None] == pool_ids[None, :]).astype(jnp.bfloat16)
+        pick = jnp.concatenate([home_back, pool_back, shared_hidden], axis=1)
+        source = jnp.concatenate(
+            [home_ret.reshape(-1, model_width), pool_ret.reshape(-1, model_width), shared_down],
+            axis=0,
+        )
+        return jnp.dot(pick, source, preferred_element_type=jnp.float32)
 
     def all_served():
         return combined().astype(jnp.bfloat16)

time: 196 us -> 149 us (0.76)
  Pallas kernels: 177 us -> 144 us
  other arithmetic: 9.05 us -> 0 us
  matrix products: 4.05 us -> 0 us
    pallas_call x1, Pallas kernels: 177 us -> 144 us  [slab_exchange(): pl.pallas_call(functools.partial(slab_kernel, dps, experts, groups, direc...]
    dot_general x1 -> x0, matrix products: 4.05 us -> none  [combined(): jnp.dot(shared_hidden, shared_down, preferred_element_type=jnp.float32)]
    select_n x4 -> x0, other arithmetic: 3.42 us -> none  [the longest x1 1.33 us: body(): back_cell = jnp.where(kept & ~left, served * stride + spot, -1)]
    unnamed x6 -> x13, local copies, waits for them, and re-layouts: 0.01 us -> 3.42 us
    convert_element_type x4 -> x0, other arithmetic: 2.99 us -> none  [the longest x1 0.81 us: body(): back = (back_cell[:, None] == back_ids[None, :]).astype(jnp.bfloat16)]
    broadcast_in_dim x3 -> x0, local copies, waits for them, and re-layouts: 2.78 us -> none  [the longest x1 1.22 us: body(): unserved = jnp.broadcast_to(jnp.max(left.astype(jnp.int32)), (8, 128))]
where the time goes in v1:
time: 149 us
  Pallas kernels  144 us (97%)
  local copies, waits for them, and re-layouts  3.42 us (2%)
    pallas_call x1, Pallas kernels, slab_exchange(): pl.pallas_call(functools.partial(slab_kernel, dps, experts, groups, direc...  144 us
    unnamed x13, local copies, waits for them, and re-layouts  3.42 us

profile of v1, /device:TPU:0, one launch (start us, length us, event | category | flops | bytes accessed | tf_op | source)
XLA Modules:
  0.0 148.5 jit_solution(10823875915907600229)
XLA Ops:
  0.0 0.0 copy-start
  0.0 0.0 copy-start.3
  0.0 0.0 copy-start.6
  0.0 0.0 copy-start.7
  0.0 0.0 copy-start.8
  0.0 0.0 copy-start.9
  0.0 144.1 %slab_moe.1 = (bf16[256,5120]{1,0:T(8,128)(2,1)}, f32[1,1]{1,0:T(1,128)}) custom-call(s32[1,256]{1,0:T(1,128)} %bitcast.36, s32[1,256]{1,0:T(1,128)} %bitcast.37, s32[1,256]{1,0:T(1,128)} %bitcast.38, f32[1,256]{1,0:T(1,128)} %bitcast.39, s32[8,32]{1,0:T(8,128)} %table_ref.1, bf16[256,5120]{1,0:T(8,128)(2,1)} %tok_ref.1, bf16[5120,256]{1,0:T(8,128)(2,1)} %bitcast.29, ...), custom_call_target="tpu_custom_call" | custom-call | tf_op jit(solution)/shard_map/slab_moe/pallas_call | solution.py:869
  144.8 0.0 copy-done
  144.8 0.0 copy-done.3
  144.8 0.0 copy-done.6
  144.8 0.0 copy-done.7
  144.9 0.0 copy-done.8
  144.9 0.0 copy-done.9
  144.9 0.2 conditional.1
  145.1 3.4 %copy.28 = bf16[256,5120]{1,0:T(8,128)(2,1)} copy(bf16[256,5120]{1,0:T(8,128)(2,1)} %get-tuple-element.52) | data formatting | bytes 5242880
Async XLA Ops:
  0.0 144.8 %copy-start = (s32[8,32]{1,0:T(8,128)S(1)}, s32[8,32]{1,0:T(8,128)}, u32[]{:S(2)}) copy-start(s32[8,32]{1,0:T(8,128)} %table_ref.1) | copy-start | bytes 3076
  0.0 144.8 %copy-start.3 = (bf16[5120,64]{0,1:T(8,128)(2,1)S(1)}, bf16[5120,64]{0,1:T(8,128)(2,1)}, u32[]{:S(2)}) copy-start(bf16[5120,64]{0,1:T(8,128)(2,1)} %param.24) | copy-start | bytes 1966084
  0.0 144.8 %copy-start.6 = (s32[256]{0:T(256)S(1)}, s32[256]{0:T(256)}, u32[]{:S(2)}) copy-start(s32[256]{0:T(256)} %param.16) | copy-start | bytes 3076
  0.0 144.8 %copy-start.7 = (s32[256]{0:T(256)S(1)}, s32[256]{0:T(256)}, u32[]{:S(2)}) copy-start(s32[256]{0:T(256)} %param.17) | copy-start | bytes 3076
  0.0 144.8 %copy-start.8 = (s32[256]{0:T(256)S(1)}, s32[256]{0:T(256)}, u32[]{:S(2)}) copy-start(s32[256]{0:T(256)} %param.18) | copy-start | bytes 3076
  0.0 144.9 %copy-start.9 = (f32[256]{0:T(256)S(1)}, f32[256]{0:T(256)}, u32[]{:S(2)}) copy-start(f32[256]{0:T(256)} %param.15) | copy-start | bytes 3076

commit v2 on v1

--- a/solution.py
+++ b/solution.py
@@ -375,6 +375,7 @@
     sd_hbm,
     out_ref,
     need_max,
+    need_part,
     need_all,
     back,
     shared_slab,
@@ -395,6 +396,8 @@
     own_sem,
     ns_sem,
     nr_sem,
+    ds_sem,
+    dr_sem,
     hs_sem,
     hr_sem,
     rs_sem,
@@ -419,8 +422,6 @@
     g = e // 2
     p = e - 2 * g
     partner = e + 1 - 2 * p
-    total = dps * experts
-    me = my_dp * experts + e
     members = 2 * dps
     j = p * dps + my_dp
     half = groups // 2
@@ -440,15 +441,18 @@
 
     barrier = pltpu.get_barrier_semaphore()
 
-    @pl.loop(1, total)
-    def _(k):
-        there = lax.rem(me + k, total)
-        pl.semaphore_signal(
-            barrier,
-            inc=1,
-            device_id={"dp": there // experts, "expert": lax.rem(there, experts)},
-            device_id_type=MESH,
-        )
+    @pl.loop(1, experts)
+    def _(k):
+        there = {"expert": flip(e, k, experts)}
+        pl.semaphore_signal(barrier, inc=1, device_id=there, device_id_type=MESH)
+
+    def peer(k):
+        m = flip(j, k, members)
+        return m, {"dp": lax.rem(m, dps), "expert": 2 * g + m // dps}
+
+    strangers = [k for k in range(1, members) if k != dps]
+    for k in strangers:
+        pl.semaphore_signal(barrier, inc=1, device_id=peer(k)[1], device_id_type=MESH)
 
     def columns(member, at=0, count=ncols):
         return pl.ds(pl.multiple_of(member * ncols + at, 128), count)
@@ -477,9 +481,13 @@
         )
 
     def n_copy(k):
-        there = lax.rem(me + k, total)
-        to = {"dp": there // experts, "expert": lax.rem(there, experts)}
-        return remote(need_all.at[me], need_all.at[me], ns_sem.at[k], nr_sem.at[k], to)
+        there = {"expert": flip(e, k, experts)}
+        return remote(need_part.at[e], need_part.at[e], ns_sem.at[k], nr_sem.at[k], there)
+
+    def d_copy(k):
+        there = {"dp": flip(my_dp, k, dps)}
+        part = need_all.at[my_dp]
+        return remote(part, part, ds_sem.at[k], dr_sem.at[k], there)
 
     def z_copy(k):
         to = flip(g, k, groups)
@@ -503,10 +511,6 @@
     def r_copy(k):
         origin = flip(e, k, experts)
         return remote(res.at[origin], ret.at[e], rs_sem.at[k], rr_sem.at[k], {"expert": origin})
-
-    def peer(k):
-        m = flip(j, k, members)
-        return m, {"dp": lax.rem(m, dps), "expert": 2 * g + m // dps}
 
     def l_copy(k):
         return remote(sel_all.at[j], sel_all.at[j], ls_sem.at[k], lr_sem.at[k], peer(k)[1])
@@ -593,7 +597,7 @@
             pool_out[to] = rows_of(pool_cell, to * pooled, pooled)
 
     with jax.named_scope("barrier"):
-        pl.semaphore_wait(barrier, total - 1)
+        pl.semaphore_wait(barrier, experts - 1 + len(strangers))
 
     for k in (3 - mid, 2 + mid, 1):
         z_copy(k).start()
@@ -623,7 +627,7 @@
         cell = jnp.where(placed, served * stride + spot, -1)
         back[...] = jnp.transpose(marks_of(experts * stride, cell)).astype(bf16)
         missed = jnp.max(jnp.where(left, 1.0, 0.0), axis=1, keepdims=True)
-        need_all[me] = jnp.broadcast_to(missed, need_all.shape[1:])
+        need_part[e] = jnp.broadcast_to(missed, need_part.shape[1:])
 
     for copy in own[1:]:
         copy.start()
@@ -644,7 +648,7 @@
     own[0].start()
     pool_relay(1)
 
-    @pl.loop(1, total)
+    @pl.loop(1, experts)
     def _(k):
         n_copy(k).start()
 
@@ -706,7 +710,7 @@
         for c in which:
             s_copy(g, c, 1, far_mid).start()
 
-    far_start(*range(min(2, len(chunks))))
+    far_start(0)
 
     def slab_step(*which):
         @pl.when(is_mid)
@@ -726,6 +730,8 @@
         def _(i):
             r_copy(experts - i).wait_recv()
 
+    far_start(*range(1, min(2, len(chunks))))
+
     with jax.named_scope("find"):
         found = jnp.dot(
             back[...], ret[...].reshape(-1, hid), preferred_element_type=jnp.float32
@@ -753,11 +759,10 @@
     def project(m, c):
         at, count = chunks[c]
         w = slab[:, :, :, at : at + count].reshape(experts * hid, count)
-        y = jnp.dot(spread[m], w, preferred_element_type=jnp.float32)
-        y += jnp.dot(
-            sel_all[m], shared_slab[:, at : at + count], preferred_element_type=jnp.float32
-        )
-        stage[m, :, at : at + count] = y.astype(jnp.bfloat16)
+        y = jnp.dot(spread[m], w, preferred_element_type=jnp.float32).astype(bf16)
+        common = shared_slab[:, at : at + count]
+        common = jnp.dot(sel_all[m], common, preferred_element_type=jnp.float32)
+        stage[m, :, at : at + count] = (y.astype(jnp.float32) + common).astype(bf16)
 
     with jax.named_scope("expand"):
         expand(j)
@@ -771,15 +776,25 @@
         with jax.named_scope("expand"):
             expand(peer(k)[0])
 
+    hidden_arrive(1)
+    hidden_arrive(2)
+    for k in range(4, members, 2):
+        hidden_arrive(k)
+    slab_step(0)
     far_start(*range(2, min(3, len(chunks))))
-    for k in [1, *range(2, members, 2)]:
-        hidden_arrive(k)
-        if k == 2:
-            far_start(*range(3, min(4, len(chunks))))
-            slab_step(0)
-    far_start(*range(4, len(chunks)))
     for k in range(3, members, 2):
         hidden_arrive(k)
+    slab_step(1)
+
+    @pl.loop(1, experts)
+    def _(k):
+        n_copy(k).wait_recv()
+
+    need_all[my_dp] = jnp.max(need_part[...], axis=0)
+
+    @pl.loop(1, dps)
+    def _(k):
+        d_copy(k).start()
 
     def own_out(c):
         at, count = chunks[c]
@@ -793,17 +808,21 @@
         with jax.named_scope("slab_arrive"):
             slab_arrive(c)
 
-        @pl.loop(1, members)
-        def _(i):
+        def send_out(i):
             k = members - i
             with jax.named_scope("project"):
                 project(peer(k)[0], c)
             o_copy(k, c).start()
 
+        pl.loop(1, members // 2)(send_out)
+        if c < 2:
+            far_start(*range(3 + c, min(4 + c, len(chunks)) if c == 0 else len(chunks)))
+        pl.loop(members // 2, members)(send_out)
+
         project(j, c)
         own_out(c).start()
-        if c + 1 < len(chunks):
-            slab_step(c + 1)
+        if c + 2 < len(chunks):
+            slab_step(c + 2)
 
     for c in range(len(chunks)):
 
@@ -832,9 +851,13 @@
     def _(k):
         z_copy(k).wait_send()
 
-    @pl.loop(1, total)
-    def _(k):
-        n_copy(k).wait()
+    @pl.loop(1, experts)
+    def _(k):
+        n_copy(k).wait_send()
+
+    @pl.loop(1, dps)
+    def _(k):
+        d_copy(k).wait()
 
     @pl.loop(1, members)
     def _(k):
@@ -875,7 +898,8 @@
         in_specs=[vmem] * 6 + [anywhere] * 3 + [vmem] * 2 + [anywhere],
         out_specs=(vmem, pl.BlockSpec(memory_space=pltpu.SMEM)),
         scratch_shapes=[
-            pltpu.VMEM((dps * experts, 8, 128), jnp.float32),
+            pltpu.VMEM((experts, 8, 128), jnp.float32),
+            pltpu.VMEM((dps, 8, 128), jnp.float32),
             pltpu.VMEM((rows, experts * cell), bf16),
             pltpu.VMEM((128, ncols), bf16),
             pltpu.VMEM((experts, direct, width), bf16),
@@ -894,7 +918,8 @@
             dma((3,)),
             dma((3,)),
         ]
-        + [dma((dps * experts,))] * 2
+        + [dma((experts,))] * 2
+        + [dma((dps,))] * 2
         + [dma((experts,))] * 4
         + [dma((groups,))] * 4
         + [dma((members,))] * 4
@@ -916,6 +941,32 @@
     )
 
 
+def hand_over_kernel(parts, src, dst, sem):
+    rows = src.shape[0] // parts
+
+    def copy(i):
+        here = pl.ds(i * rows, rows)
+        return pltpu.make_async_copy(src.at[here], dst.at[here], sem.at[i])
+
+    for i in range(parts):
+        copy(i).start()
+    for i in range(parts):
+        copy(i).wait()
+
+
+def hand_over(values):
+    parts = 4
+    return pl.pallas_call(
+        functools.partial(hand_over_kernel, parts),
+        out_shape=jax.ShapeDtypeStruct(values.shape, values.dtype),
+        in_specs=[pl.BlockSpec(memory_space=pltpu.VMEM)],
+        out_specs=pl.BlockSpec(memory_space=pl.ANY),
+        scratch_shapes=[pltpu.SemaphoreType.DMA((parts,))],
+        compiler_params=pltpu.CompilerParams(vmem_limit_bytes=4 * 1024 * 1024),
+        name="hand_over",
+    )(values)
+
+
 def slab_body(direct, pooled, args):
     tokens, router_logit, expert_id, token_slot, keep, table = args[:6]
     weights = tuple(w[0] for w in args[6:9])
@@ -972,7 +1023,7 @@
         common = jnp.dot(hidden, shared_down, preferred_element_type=jnp.float32)
         return jnp.where(left[:, None], (common + rest).astype(jnp.bfloat16), out)
 
-    return lax.cond(need[0, 0] > 0, some_left, lambda: out)
+    return lax.cond(need[0, 0] > 0, some_left, lambda: hand_over(out))
 
 
 def body(

time: 149 us -> 138 us (0.926)
  Pallas kernels: 144 us -> 137 us
  local copies, waits for them, and re-layouts: 3.42 us -> 0.02 us
    pallas_call x1, Pallas kernels: 144 us -> 136 us  [slab_exchange(): pl.pallas_call(functools.partial(slab_kernel, dps, experts, groups, direc...]
    unnamed x13 -> x12, local copies, waits for them, and re-layouts: 3.42 us -> 0.02 us
    pallas_call x0 -> x1, Pallas kernels: none -> 1.52 us  [hand_over(): pl.pallas_call(functools.partial(hand_over_kernel, parts), out_shape=jax....]
where the time goes in v2:
time: 138 us
  Pallas kernels  137 us (99%)
    pallas_call x1, Pallas kernels, slab_exchange(): pl.pallas_call(functools.partial(slab_kernel, dps, experts, groups, direc...  136 us

profile of v2, /device:TPU:0, one launch (start us, length us, event | category | flops | bytes accessed | tf_op | source)
XLA Modules:
  0.0 138.0 jit_solution(11522696217858497748)
XLA Ops:
  0.0 0.0 copy-start
  0.0 0.0 copy-start.4
  0.0 0.0 copy-start.7
  0.0 0.0 copy-start.8
  0.0 0.0 copy-start.9
  0.0 0.0 copy-start.10
  0.0 135.6 %slab_moe.1 = (bf16[256,5120]{1,0:T(8,128)(2,1)S(1)}, f32[1,1]{1,0:T(1,128)}) custom-call(s32[1,256]{1,0:T(1,128)} %bitcast.36, s32[1,256]{1,0:T(1,128)} %bitcast.37, s32[1,256]{1,0:T(1,128)} %bitcast.38, f32[1,256]{1,0:T(1,128)} %bitcast.39, s32[8,32]{1,0:T(8,128)} %table_ref.1, bf16[256,5120]{1,0:T(8,128)(2,1)} %tok_ref.1, bf16[5120,256]{1,0:T(8,128)(2,1)} %bitcast.29, ...), custom_call_target="tpu_custom_call" | custom-call | tf_op jit(solution)/shard_map/slab_moe/pallas_call | solution.py:892
  136.3 0.0 copy-done
  136.3 0.0 copy-done.4
  136.3 0.0 copy-done.7
  136.3 0.0 copy-done.8
  136.3 0.0 copy-done.9
  136.3 0.0 copy-done.10
  136.3 1.5 %conditional.1 = (bf16[256,5120]{1,0:T(8,128)(2,1)}) conditional(s32[]{:T(128)} %bitcast.13, bf16[256,5120]{1,0:T(8,128)(2,1)S(1)} %get-tuple-element.51, (s32[256]{0:T(256)S(1)}, s32[256]{0:T(256)S(1)}, s32[256]{0:T(256)S(1)}, s32[8,32]{1,0:T(8,128)S(1)}, bf16[256,5120]{1,0:T(8,128)(2,1)}, /*index=5*/bf16[5120,64]{0,1:T(8,128)(2,1)}, ...), branch_computations={%region_0.0_spmd, %region_1.5_spmd} | conditional | flops 6558306816 | bytes 187229120 | solution.py:1026
  136.3 1.5 %hand_over.1 = bf16[256,5120]{1,0:T(8,128)(2,1)} custom-call(bf16[256,5120]{1,0:T(8,128)(2,1)S(1)} %src), custom_call_target="tpu_custom_call" | custom-call | tf_op jit(solution)/shard_map/cond/branch_0_fun/hand_over/pallas_call | solution.py:959
Async XLA Ops:
  0.0 136.3 %copy-start = (s32[8,32]{1,0:T(8,128)S(1)}, s32[8,32]{1,0:T(8,128)}, u32[]{:S(2)}) copy-start(s32[8,32]{1,0:T(8,128)} %table_ref.1) | copy-start | bytes 3076
  0.0 136.3 %copy-start.4 = (bf16[5120,64]{0,1:T(8,128)(2,1)S(1)}, bf16[5120,64]{0,1:T(8,128)(2,1)}, u32[]{:S(2)}) copy-start(bf16[5120,64]{0,1:T(8,128)(2,1)} %param.24) | copy-start | bytes 1966084
  0.0 136.3 %copy-start.7 = (s32[256]{0:T(256)S(1)}, s32[256]{0:T(256)}, u32[]{:S(2)}) copy-start(s32[256]{0:T(256)} %param.16) | copy-start | bytes 3076
  0.0 136.3 %copy-start.8 = (s32[256]{0:T(256)S(1)}, s32[256]{0:T(256)}, u32[]{:S(2)}) copy-start(s32[256]{0:T(256)} %param.17) | copy-start | bytes 3076
  0.0 136.3 %copy-start.9 = (s32[256]{0:T(256)S(1)}, s32[256]{0:T(256)}, u32[]{:S(2)}) copy-start(s32[256]{0:T(256)} %param.18) | copy-start | bytes 3076
  0.0 136.3 %copy-start.10 = (f32[256]{0:T(256)S(1)}, f32[256]{0:T(256)}, u32[]{:S(2)}) copy-start(f32[256]{0:T(256)} %param.15) | copy-start | bytes 3076

commit v3 on v2

--- a/solution.py
+++ b/solution.py
@@ -366,15 +366,18 @@
     keep_ref,
     logit_ref,
     table_ref,
-    tok_ref,
+    tok_hbm,
     wg_hbm,
     wu_hbm,
     wd_hbm,
-    sg_ref,
-    su_ref,
+    sg_hbm,
+    su_hbm,
     sd_hbm,
     out_ref,
     need_max,
+    tok_ref,
+    sg_ref,
+    su_ref,
     need_part,
     need_all,
     back,
@@ -392,6 +395,7 @@
     h_all,
     spread,
     stage,
+    in_sem,
     w_sem,
     own_sem,
     ns_sem,
@@ -434,7 +438,7 @@
     hid = wg.shape[1]
     mix = sg_ref.shape[0]
     spill = table_ref.shape[1]
-    base = (direct + 15) // 16 * 16
+    base = (direct + 7) // 8 * 8
     stride = base + pooled
     ncols = slab.shape[3]
     chunks = split_columns(ncols)
@@ -545,10 +549,16 @@
         part = slab.at[block, :, :, pl.ds(at, count)]
         return remote(part, part, ss_sem.at[slot, c], sr_sem.at[block, c], {"expert": 2 * to + p})
 
-    for copy in weights:
+    inputs = [
+        pltpu.make_async_copy(a, b, in_sem.at[i])
+        for i, (a, b) in enumerate(((tok_hbm, tok_ref), (sg_hbm, sg_ref), (su_hbm, su_ref)))
+    ]
+    for copy in inputs:
         copy.start()
     own_slab.start()
     own_mix.start()
+    for copy in weights:
+        copy.start()
 
     bf16 = jnp.bfloat16
 
@@ -591,17 +601,25 @@
         chosen = jnp.dot(pick.astype(bf16), tok_ref[...], preferred_element_type=jnp.float32)
         return (chosen * factor).astype(bf16)
 
-    @pl.loop(0, groups)
-    def _(to):
+    with jax.named_scope("tok_wait"):
+        inputs[0].wait()
+
+    def pack_pool(k):
+        to = flip(g, k, groups)
         with jax.named_scope("pack_pool"):
             pool_out[to] = rows_of(pool_cell, to * pooled, pooled)
 
+    pack_pool(3 - mid)
+    pack_pool(2 + mid)
+
     with jax.named_scope("barrier"):
         pl.semaphore_wait(barrier, experts - 1 + len(strangers))
 
-    for k in (3 - mid, 2 + mid, 1):
-        z_copy(k).start()
-
+    z_copy(3 - mid).start()
+    z_copy(2 + mid).start()
+    pack_pool(1)
+    z_copy(1).start()
+    pack_pool(0)
     v_copy().start()
 
     @pl.loop(0, experts)
@@ -611,6 +629,8 @@
             home_out[to] = rows_of(home_cell, to * direct, direct)
 
     with jax.named_scope("shared"):
+        inputs[1].wait()
+        inputs[2].wait()
         tok = tok_ref[...]
         last = (((1,), (1,)), ((), ()))
         shared_gate = lax.dot_general(tok, sg_ref[...], last, preferred_element_type=jnp.float32)
@@ -712,10 +732,10 @@
 
     far_start(0)
 
-    def slab_step(*which):
+    def relay(c):
         @pl.when(is_mid)
         def _():
-            for c in which:
+            if c < len(chunks):
                 with jax.named_scope("slab_relay"):
                     for slot, block in ((2, far_mid), (3, far_end)):
                         copy = s_copy(block, c, slot, mate)
@@ -777,14 +797,13 @@
             expand(peer(k)[0])
 
     hidden_arrive(1)
-    hidden_arrive(2)
-    for k in range(4, members, 2):
+    for k in range(2, members, 2):
         hidden_arrive(k)
-    slab_step(0)
+    relay(0)
     far_start(*range(2, min(3, len(chunks))))
     for k in range(3, members, 2):
         hidden_arrive(k)
-    slab_step(1)
+    relay(1)
 
     @pl.loop(1, experts)
     def _(k):
@@ -804,7 +823,61 @@
             os_sem.at[0, c],
         )
 
+    def finish_out(c):
+        @pl.loop(1, members)
+        def _(k):
+            with jax.named_scope("out_wait"):
+                o_copy(k, c).wait()
+
+        own_out(c).wait()
+
+    def finish_sends():
+        v_copy().wait_send()
+        for c in range(len(chunks)):
+            s_copy(g, c, 0, mate).wait_send()
+            if c + 1 < len(chunks):
+                s_copy(g, c, 1, far_mid).wait_send()
+
+        @pl.loop(0, groups)
+        def _(k):
+            x_copy(k).wait_send()
+
+        @pl.loop(1, groups)
+        def _(k):
+            z_copy(k).wait_send()
+
+        @pl.loop(1, members)
+        def _(k):
+            l_copy(k).wait_send()
+
+        for k in range(1, members):
+            g_copy(k).wait_send()
+
+        @pl.loop(1, experts)
+        def _(k):
+            n_copy(k).wait_send()
+            h_copy(k).wait_send()
+            r_copy(k).wait_send()
+
+        @pl.loop(1, dps)
+        def _(k):
+            d_copy(k).wait()
+
+    def finish_relays():
+        s_copy(g, len(chunks) - 1, 1, far_mid).wait_send()
+
+        @pl.when(is_mid)
+        def _():
+            for c in range(len(chunks)):
+                for slot, block in ((2, far_mid), (3, far_end)):
+                    s_copy(block, c, slot, mate).wait_send()
+
     for c in range(len(chunks)):
+        if c == len(chunks) - 1:
+            with jax.named_scope("drain"):
+                finish_sends()
+                for early in range(max(0, len(chunks) - 3)):
+                    finish_out(early)
         with jax.named_scope("slab_arrive"):
             slab_arrive(c)
 
@@ -821,55 +894,12 @@
 
         project(j, c)
         own_out(c).start()
-        if c + 2 < len(chunks):
-            slab_step(c + 2)
-
-    for c in range(len(chunks)):
-
-        @pl.loop(1, members)
-        def _(k):
-            with jax.named_scope("out_wait"):
-                o_copy(k, c).wait()
-
-        own_out(c).wait()
-        s_copy(g, c, 1, far_mid).wait_send()
-        s_copy(g, c, 0, mate).wait_send()
-
-        @pl.when(is_mid)
-        def _():
-            for slot, block in ((2, far_mid), (3, far_end)):
-                s_copy(block, c, slot, mate).wait_send()
-
-    with jax.named_scope("v_wait"):
-        v_copy().wait_send()
-
-    @pl.loop(0, groups)
-    def _(k):
-        x_copy(k).wait_send()
-
-    @pl.loop(1, groups)
-    def _(k):
-        z_copy(k).wait_send()
-
-    @pl.loop(1, experts)
-    def _(k):
-        n_copy(k).wait_send()
-
-    @pl.loop(1, dps)
-    def _(k):
-        d_copy(k).wait()
-
-    @pl.loop(1, members)
-    def _(k):
-        l_copy(k).wait_send()
-
-    for k in range(1, members):
-        g_copy(k).wait_send()
-
-    @pl.loop(1, experts)
-    def _(k):
-        h_copy(k).wait_send()
-        r_copy(k).wait_send()
+        relay(c + 2)
+
+    finish_relays()
+
+    for c in range(max(0, len(chunks) - 3), len(chunks)):
+        finish_out(c)
 
     need_max[0, 0] = jnp.max(need_all[...])
 
@@ -884,7 +914,7 @@
     members = 2 * dps
     ncols = width // members
     parts = len(split_columns(ncols))
-    cell = (direct + 15) // 16 * 16 + pooled
+    cell = (direct + 7) // 8 * 8 + pooled
     bf16 = jnp.bfloat16
     vmem = pl.BlockSpec(memory_space=pltpu.VMEM)
     anywhere = pl.BlockSpec(memory_space=pl.ANY)
@@ -895,9 +925,12 @@
             jax.ShapeDtypeStruct((rows, width), bf16),
             jax.ShapeDtypeStruct((1, 1), jnp.float32),
         ),
-        in_specs=[vmem] * 6 + [anywhere] * 3 + [vmem] * 2 + [anywhere],
+        in_specs=[vmem] * 5 + [anywhere] * 7,
         out_specs=(vmem, pl.BlockSpec(memory_space=pltpu.SMEM)),
         scratch_shapes=[
+            pltpu.VMEM((rows, width), bf16),
+            pltpu.VMEM(shared[0].shape[::-1], bf16),
+            pltpu.VMEM(shared[1].shape[::-1], bf16),
             pltpu.VMEM((experts, 8, 128), jnp.float32),
             pltpu.VMEM((dps, 8, 128), jnp.float32),
             pltpu.VMEM((rows, experts * cell), bf16),
@@ -915,6 +948,7 @@
             pltpu.VMEM((members, rows, hid), bf16),
             pltpu.VMEM((members, rows, experts * hid), bf16),
             pltpu.VMEM((members, rows, ncols), bf16),
+            dma((3,)),
             dma((3,)),
             dma((3,)),
         ]

time: 138 us -> 138 us (level)
  no operation moved by 1% of the time
where the time goes in v3:
time: 138 us
  Pallas kernels  137 us (99%)
    pallas_call x1, Pallas kernels, slab_exchange(): pl.pallas_call(functools.partial(slab_kernel, dps, experts, groups, direc...  135 us

profile of v3, /device:TPU:0, one launch (start us, length us, event | category | flops | bytes accessed | tf_op | source)
XLA Modules:
  0.0 137.7 jit_solution(15278471451755107359)
XLA Ops:
  0.0 0.0 copy-start
  0.0 0.0 copy-start.4
  0.0 0.0 copy-start.7
  0.0 0.0 copy-start.8
  0.0 0.0 copy-start.9
  0.0 0.0 copy-start.10
  0.0 135.3 %slab_moe.1 = (bf16[256,5120]{1,0:T(8,128)(2,1)S(1)}, f32[1,1]{1,0:T(1,128)}) custom-call(s32[1,256]{1,0:T(1,128)} %bitcast.36, s32[1,256]{1,0:T(1,128)} %bitcast.37, s32[1,256]{1,0:T(1,128)} %bitcast.38, f32[1,256]{1,0:T(1,128)} %bitcast.39, s32[8,32]{1,0:T(8,128)} %table_ref.1, bf16[256,5120]{1,0:T(8,128)(2,1)} %tok_hbm.1, bf16[5120,256]{1,0:T(8,128)(2,1)} %bitcast.29, ...), custom_call_target="tpu_custom_call" | custom-call | tf_op jit(solution)/shard_map/slab_moe/pallas_call | solution.py:922
  136.0 0.0 copy-done
  136.0 0.0 copy-done.4
  136.0 0.0 copy-done.7
  136.0 0.0 copy-done.8
  136.0 0.0 copy-done.9
  136.0 0.0 copy-done.10
  136.0 1.5 %conditional.1 = (bf16[256,5120]{1,0:T(8,128)(2,1)}) conditional(s32[]{:T(128)} %bitcast.13, bf16[256,5120]{1,0:T(8,128)(2,1)S(1)} %get-tuple-element.51, (s32[256]{0:T(256)S(1)}, s32[256]{0:T(256)S(1)}, s32[256]{0:T(256)S(1)}, s32[8,32]{1,0:T(8,128)S(1)}, bf16[256,5120]{1,0:T(8,128)(2,1)}, /*index=5*/bf16[5120,64]{0,1:T(8,128)(2,1)}, ...), branch_computations={%region_0.0_spmd, %region_1.5_spmd} | conditional | flops 6558306816 | bytes 187229120 | solution.py:1060
  136.0 1.5 %hand_over.1 = bf16[256,5120]{1,0:T(8,128)(2,1)} custom-call(bf16[256,5120]{1,0:T(8,128)(2,1)S(1)} %src), custom_call_target="tpu_custom_call" | custom-call | tf_op jit(solution)/shard_map/cond/branch_0_fun/hand_over/pallas_call | solution.py:993
Async XLA Ops:
  0.0 136.0 %copy-start = (s32[8,32]{1,0:T(8,128)S(1)}, s32[8,32]{1,0:T(8,128)}, u32[]{:S(2)}) copy-start(s32[8,32]{1,0:T(8,128)} %table_ref.1) | copy-start | bytes 3076
  0.0 136.0 %copy-start.4 = (bf16[5120,64]{0,1:T(8,128)(2,1)S(1)}, bf16[5120,64]{0,1:T(8,128)(2,1)}, u32[]{:S(2)}) copy-start(bf16[5120,64]{0,1:T(8,128)(2,1)} %param.24) | copy-start | bytes 1966084
  0.0 136.0 %copy-start.7 = (s32[256]{0:T(256)S(1)}, s32[256]{0:T(256)}, u32[]{:S(2)}) copy-start(s32[256]{0:T(256)} %param.16) | copy-start | bytes 3076
  0.0 136.0 %copy-start.8 = (s32[256]{0:T(256)S(1)}, s32[256]{0:T(256)}, u32[]{:S(2)}) copy-start(s32[256]{0:T(256)} %param.17) | copy-start | bytes 3076
  0.0 136.0 %copy-start.9 = (s32[256]{0:T(256)S(1)}, s32[256]{0:T(256)}, u32[]{:S(2)}) copy-start(s32[256]{0:T(256)} %param.18) | copy-start | bytes 3076
  0.0 136.0 %copy-start.10 = (f32[256]{0:T(256)S(1)}, f32[256]{0:T(256)}, u32[]{:S(2)}) copy-start(f32[256]{0:T(256)} %param.15) | copy-start | bytes 3076
